TPU v7x, 32 devices: a whole 2x2x4 slice. The times are simulated.
32 devices in a mesh: layer: 4 (over y, x), latent: 8 (over z, core).
Axes of the slice: x: 2, y: 2, z: 4, core: 2. Of those that a mesh axis runs over, the one named last changes fastest.
Arguments:
- tokens: bfloat16 [128, 16384], P('latent', 'layer'), may hold values from -6 to 6
- encoder_weight: bfloat16 [16384, 16384], P('layer', 'latent'), may hold values from -0.046875 to 0.046875
- encoder_bias: float32 [16384], P('latent'), may hold values from -3 to 3, as said below
- decoder_weight: bfloat16 [16384, 16384], P('latent', 'layer'), may hold values from -2 to 2
- decoder_bias: float32 [16384], P('layer'), may hold values from -12 to 12
Outputs:
- encoder_grad: bfloat16 [16384, 16384], P('layer', 'latent')
- decoder_grad: bfloat16 [16384, 16384], P('latent', 'layer')
Inputs may be any that keep to these rules, and one draw needn't show every extreme that they name: `encoder_bias`: mean about -0.5.
All inputs are finite; a program needn't handle non-finite values.
Results may differ from a plain program's by a relative error of at most 0.0059.
Values may be sent and summed in bfloat16 or wider, within the bound.
No kernel may reach another device: no remote copies, remote signals or barrier semaphores. Data moves between devices by JAX's collectives and lax.ppermute only.
A program may use at most 128 MiB of HBM per device.

v0:
```python
import jax
import jax.numpy as jnp
from jax import lax
from jax.sharding import PartitionSpec as P

L = 4
D = 4096


LOSS_SCALE = 0.0625
SPARSITY = 0.5
sharpness = 4.0
epsilon = 1e-06


def shards(tokens, encoder_weight, encoder_bias, decoder_weight, decoder_bias):
    rows_dev, width_dev = tokens.shape
    latents_dev = encoder_weight.shape[1]
    groups = lax.axis_size("layer")
    layer_index = lax.axis_index("layer") * width_dev // D
    wide = decoder_weight.astype(jnp.float32)
    squares_own = jnp.sum(wide * wide, axis=1)
    placed = jnp.where(jnp.arange(L)[:, None] == layer_index, squares_own[None, :], 0.0)
    squares = lax.psum(placed, "layer")
    row_norms = jnp.sqrt(squares + epsilon)
    weights_sum = jnp.sum(row_norms, axis=0)
    own_norm = lax.dynamic_slice_in_dim(row_norms, layer_index, 1, 0)[0]
    every_token = lax.all_gather(tokens, "latent", axis=0, tiled=True)
    partial_value = jnp.dot(every_token, encoder_weight, preferred_element_type=jnp.float32)
    share_width = latents_dev // groups
    offset = lax.axis_index("layer") * share_width
    preact = lax.psum_scatter(partial_value, "layer", scatter_dimension=1, tiled=True)
    preact = preact + lax.dynamic_slice_in_dim(encoder_bias, offset, share_width, 0)[None, :]
    hidden_share = (jax.nn.softplus(sharpness * preact) / sharpness).astype(jnp.bfloat16)
    hidden = lax.all_gather(hidden_share, "layer", axis=1, tiled=True)
    slopes = jax.nn.sigmoid(sharpness * preact)
    rebuilt = lax.psum(
        jnp.dot(hidden, decoder_weight, preferred_element_type=jnp.float32), "latent"
    )
    errors = rebuilt + decoder_bias[None, :] - every_token.astype(jnp.float32)
    error_grad = (LOSS_SCALE * errors).astype(jnp.bfloat16)
    back_terms = lax.dot_general(
        error_grad, decoder_weight, (((1,), (1,)), ((), ())), preferred_element_type=jnp.float32
    )
    summed = lax.psum_scatter(back_terms, "layer", scatter_dimension=1, tiled=True)
    penalty = lax.dynamic_slice_in_dim(weights_sum, offset, share_width, 0)
    grad_share = ((summed + LOSS_SCALE * SPARSITY * penalty[None, :]) * slopes).astype(jnp.bfloat16)
    pre_grad = lax.all_gather(grad_share, "layer", axis=1, tiled=True)
    encoder_grad = lax.dot_general(
        every_token, pre_grad, (((0,), (0,)), ((), ())), preferred_element_type=jnp.float32
    ).astype(jnp.bfloat16)
    totals = jnp.sum(hidden.astype(jnp.float32), axis=0)
    direct = lax.dot_general(
        hidden, error_grad, (((0,), (0,)), ((), ())), preferred_element_type=jnp.float32
    )
    sparse_term = wide * (LOSS_SCALE * SPARSITY * totals / own_norm)[:, None]
    decoder_grad = (direct + sparse_term).astype(jnp.bfloat16)
    return (encoder_grad, decoder_grad)


def solution(mesh):
    placed = (
        P("latent", "layer"),
        P("layer", "latent"),
        P("latent"),
        P("latent", "layer"),
        P("layer"),
    )
    return jax.shard_map(
        shards,
        mesh=mesh,
        in_specs=placed,
        out_specs=(P("layer", "latent"), P("latent", "layer")),
        check_vma=False,
    )
```

profile of v0, /device:TPU:0, one launch (start us, length us, event | category | flops | bytes accessed | tf_op | source)
XLA Modules:
  0.0 247.9 jit_solution(9035878231300968238)
XLA Ops:
  7.2 0.7 all-gather.2.cloned.1.call-update
  7.9 26.6 %all-gather.2.cloned.1.call-done = bf16[128,4096]{1,0:T(8,128)(2,1)} async-done(((bf16[16,4096]{1,0:T(8,128)(2,1)}), bf16[128,4096]{1,0:T(8,128)(2,1)}) %all-gather.2.cloned.1.call-update) | async-done | bytes 1048592 | tf_op jit(solution)/shard_map/all_gather | solution.py:28
  34.6 9.4 %fusion.6 = f32[128,2048]{1,0:T(8,128)} fusion(bf16[128,4096]{1,0:T(8,128)(2,1)} %all-gather.2.cloned.1.call-done, bf16[4096,2048]{1,0:T(8,128)(2,1)} %param.6), kind=kOutput, calls=%fused_computation.20 | convolution fusion | flops 2147483648 | bytes 18874368 | tf_op jit(solution)/shard_map/dot_general | solution.py:29
  44.0 0.0 all-reduce.2.cloned.1.call-start
  44.1 0.8 dynamic_slice.9
  44.8 26.9 %reduce-scatter.3.cloned.1.call-done = f32[128,512]{1,0:T(8,128)} async-done(((f32[128,2048]{1,0:T(8,128)}), f32[128,512]{1,0:T(8,128)}) %reduce-scatter.3.cloned.1.call-update) | async-done | bytes 262160 | tf_op jit(solution)/shard_map/reduce_scatter | solution.py:32
  71.7 1.1 fusion.4
  72.8 10.1 %all_gather.10 = bf16[128,2048]{1,0:T(8,128)(2,1)S(1)} all-gather(bf16[128,512]{1,0:T(8,128)(2,1)S(1)} %fusion.4), channel_id=1, replica_groups=mesh['layer'=4,'latent'=8] {'layer'}, dimensions={1}, use_global_device_ids=true | all-gather | bytes 655360 | tf_op jit(solution)/shard_map/all_gather | solution.py:35
  82.9 9.5 %fusion.7 = f32[128,4096]{1,0:T(8,128)} fusion(bf16[128,2048]{1,0:T(8,128)(2,1)S(1)} %all_gather.10, bf16[2048,4096]{1,0:T(8,128)(2,1)} %param.8), kind=kOutput, calls=%fused_computation.21 | convolution fusion | flops 2147483648 | bytes 19398656 | tf_op jit(solution)/shard_map/dot_general | solution.py:38
  92.5 0.0 reduce-scatter.5.cloned.1.call-start
  92.5 7.4 %fusion = f32[2048]{0:T(1024)S(1)} fusion(bf16[2048,4096]{1,0:T(8,128)(2,1)} %param.8), kind=kLoop, calls=%fused_computation.2 | loop fusion | flops 25163776 | bytes 16785408 | tf_op jit(solution)/shard_map/reduce_sum | solution.py:22
  99.9 0.1 broadcast_select_fusion
  100.0 15.1 %psum.15 = f32[4,2048]{1,0:T(4,128)S(1)} all-reduce(f32[4,2048]{1,0:T(4,128)S(1)} %broadcast_select_fusion), channel_id=1, replica_groups=mesh['layer'=4,'latent'=8] {'layer'}, use_global_device_ids=true, to_apply=%region_4.5 | all-reduce | flops 8192 | bytes 65536 | tf_op jit(solution)/shard_map/psum | solution.py:24
  115.2 42.5 %all-reduce.2.cloned.1.call-done = f32[128,4096]{1,0:T(8,128)} async-done(((f32[128,4096]{1,0:T(8,128)}), f32[128,4096]{1,0:T(8,128)}) %all-reduce.2.cloned.1.call-update) | async-done | bytes 2097168 | tf_op jit(solution)/shard_map/psum | solution.py:37
  157.7 1.9 multiply_convert_fusion
  159.6 12.4 %fusion.8 = f32[128,2048]{1,0:T(8,128)} fusion(bf16[128,4096]{1,0:T(8,128)(2,1)S(1)} %multiply_convert_fusion, bf16[2048,4096]{1,0:T(8,128)(2,1)} %param.8), kind=kOutput, calls=%fused_computation.22 | convolution fusion | flops 2147483648 | bytes 18874368 | tf_op jit(solution)/shard_map/dot_general | solution.py:42
  172.0 0.1 dynamic-slice_multiply_fusion
  172.1 0.1 convert_reduce_fusion
  172.2 12.0 %fusion.2 = bf16[2048,4096]{1,0:T(8,128)(2,1)} fusion(bf16[2048,4096]{1,0:T(8,128)(2,1)} %param.8, f32[2048]{0:T(1024)S(1)} %multiply_divide_fusion, bf16[128,2048]{1,0:T(8,128)(2,1)S(1)} %all_gather.10, bf16[128,4096]{1,0:T(8,128)(2,1)S(1)} %multiply_convert_fusion), kind=kOutput, calls=%fused_computation.4 | convolution fusion | flops 2181038080 | bytes 35135488 | tf_op jit(solution)/shard_map/dot_general | solution.py:53
  184.2 15.5 %reduce-scatter.5.cloned.1.call-done = f32[128,512]{1,0:T(8,128)} async-done(((f32[128,2048]{1,0:T(8,128)}), f32[128,512]{1,0:T(8,128)}) %reduce-scatter.5.cloned.1.call-update) | async-done | bytes 262160 | tf_op jit(solution)/shard_map/reduce_scatter | solution.py:45
  199.7 1.0 multiply_convert_fusion.1
  200.8 10.1 %all_gather.11 = bf16[128,2048]{1,0:T(8,128)(2,1)S(1)} all-gather(bf16[128,512]{1,0:T(8,128)(2,1)S(1)} %multiply_convert_fusion.1), channel_id=1, replica_groups=mesh['layer'=4,'latent'=8] {'layer'}, dimensions={1}, use_global_device_ids=true | all-gather | bytes 655360 | tf_op jit(solution)/shard_map/all_gather | solution.py:48
  210.8 8.1 %convert_bitcast_fusion = bf16[4096,2048]{0,1:T(8,128)(2,1)} fusion(bf16[128,2048]{1,0:T(8,128)(2,1)S(1)} %all_gather.11, bf16[128,4096]{1,0:T(8,128)(2,1)S(1)} %copy-done), kind=kOutput, calls=%fused_computation.5 | convolution fusion | flops 2155872256 | bytes 18350080 | tf_op jit(solution)/shard_map/dot_general | solution.py:49
  218.9 22.4 %copy.8 = bf16[4096,2048]{1,0:T(8,128)(2,1)} copy(bf16[4096,2048]{0,1:T(8,128)(2,1)} %convert_bitcast_fusion) | data formatting | bytes 33554432
  (15 shorter events, 0.2 us)
Async XLA Ops:
  7.2 27.4 %all-gather.2.cloned.1.call-start = ((), (), s32[]{:S(2)}) async-start(), calls=%async_computation.2 | async-start | bytes 1179648 | tf_op jit(solution)/shard_map/all_gather | solution.py:28
  7.9 63.8 %reduce-scatter.3.cloned.1.call-start = ((), (), s32[]{:S(2)}) async-start(), calls=%async_computation.3 | async-start | bytes 1310720 | tf_op jit(solution)/shard_map/reduce_scatter | solution.py:32
  44.0 113.7 %all-reduce.2.cloned.1.call-start = ((), (), s32[]{:S(2)}) async-start(), calls=%async_computation.4 | async-start | bytes 4194304 | tf_op jit(solution)/shard_map/psum | solution.py:37
  82.9 74.8 %copy-start = (bf16[128,4096]{1,0:T(8,128)(2,1)S(1)}, bf16[128,4096]{1,0:T(8,128)(2,1)}, u32[]{:S(2)}) copy-start(bf16[128,4096]{1,0:T(8,128)(2,1)} %all-gather.2.cloned.1.call-done) | copy-start | bytes 3145732
  82.9 74.8 %copy-start.2 = (f32[4096]{0:T(1024)S(1)}, f32[4096]{0:T(1024)}, u32[]{:S(2)}) copy-start(f32[4096]{0:T(1024)} %param.9) | copy-start | bytes 49156
  92.5 107.3 %reduce-scatter.5.cloned.1.call-start = ((), (), s32[]{:S(2)}) async-start(), calls=%async_computation.5 | async-start | bytes 1310720 | tf_op jit(solution)/shard_map/reduce_scatter | solution.py:45
  172.2 27.5 %copy-start.1 = (f32[128,512]{1,0:T(8,128)S(1)}, f32[128,512]{1,0:T(8,128)}, u32[]{:S(2)}) copy-start(f32[128,512]{1,0:T(8,128)} %reduce-scatter.3.cloned.1.call-done) | copy-start | bytes 786436
Sparse Core Ops, SparseCore 0:
  9.6 24.9 all-gather.1
  44.1 27.5 reduce-scatter.2
  92.6 65.0 all-reduce.1
  172.1 27.5 reduce-scatter.4
where the time goes:
time: 249 us; the launch traced here: 248 us
  waiting for transfers between devices  112 us (45%)
  matrix products  51.3 us (21%)
  blocking collectives  35.3 us (14%)
  local copies, waits for them, and re-layouts  23.2 us (9%)
  between operations  13.9 us (6%)
  other arithmetic  11.7 us (5%)
    psum x1, waiting for transfers between devices, shards(): lax.psum(jnp.dot(hidden, decoder_weight, preferred_element_type=jnp.float...  42.5 us
    reduce_scatter x1, waiting for transfers between devices, shards(): lax.psum_scatter(partial_value, 'layer', scatter_dimension=1, tiled=True)  26.9 us
    all_gather x1, waiting for transfers between devices, shards(): every_token = lax.all_gather(tokens, 'latent', axis=0, tiled=True)  26.6 us
    unnamed x7, local copies, waits for them, and re-layouts  22.4 us
    reduce_scatter x1, waiting for transfers between devices, shards(): lax.psum_scatter(back_terms, 'layer', scatter_dimension=1, tiled=True)  15.5 us
    psum x1, blocking collectives, shards(): squares = lax.psum(placed, 'layer')  15.1 us
    dot_general x1, matrix products, shards(): lax.dot_general(error_grad, decoder_weight, (((1,), (1,)), ((), ())), pre...  12.4 us
    dot_general x1, matrix products, shards(): lax.dot_general(hidden, error_grad, (((0,), (0,)), ((), ())), preferred_e...  12 us
  transfers between devices with their start and end apart: 4, of which 4 were waited for; matrix products, arithmetic and copies ran while one was open for 8% of the time, Pallas kernels for 0%

commit v1 on v0

--- a/solution.py
+++ b/solution.py
@@ -1,7 +1,10 @@
 import jax
 import jax.numpy as jnp
 from jax import lax
+from jax.experimental import pallas as pl
+from jax.experimental.pallas import tpu as pltpu
 from jax.sharding import PartitionSpec as P
+
 
 L = 4
 D = 4096
@@ -13,8 +16,14 @@
 epsilon = 1e-06
 
 
-def shards(tokens, encoder_weight, encoder_bias, decoder_weight, decoder_bias):
-    rows_dev, width_dev = tokens.shape
+CHUNKS = 2
+F32 = jnp.float32
+BF16 = jnp.bfloat16
+MIB = 1024 * 1024
+
+
+def general(tokens, encoder_weight, encoder_bias, decoder_weight, decoder_bias):
+    _, width_dev = tokens.shape
     latents_dev = encoder_weight.shape[1]
     groups = lax.axis_size("layer")
     layer_index = lax.axis_index("layer") * width_dev // D
@@ -58,6 +67,469 @@
     return (encoder_grad, decoder_grad)
 
 
+def call(body, out_shape, scratch, limit, flops, nbytes, args, spaces, out_spaces, aliases=None):
+    out = pl.pallas_call(
+        body,
+        in_specs=[pl.BlockSpec(memory_space=s) for s in spaces],
+        out_specs=[pl.BlockSpec(memory_space=s) for s in out_spaces],
+        out_shape=out_shape,
+        scratch_shapes=scratch,
+        input_output_aliases=aliases or {},
+        compiler_params=pltpu.CompilerParams(vmem_limit_bytes=limit * MIB),
+        cost_estimate=pl.CostEstimate(flops=flops, bytes_accessed=nbytes, transcendentals=0),
+    )(*args)
+    return list(out)
+
+
+VMEM, ANY = pltpu.VMEM, pl.ANY
+
+
+def hold(weight, blocks, axis, chunk, chunks, behind, sums=None):
+    shape = tuple(n // chunks if i == axis else n for i, n in enumerate(weight.shape))
+    rows, wide = shape
+    step = rows // blocks
+    norms = sums is not None
+    given = [] if not norms or isinstance(sums, str) else [sums]
+    last = chunk == chunks - 1
+
+    def body(w_hbm, *refs):
+        refs = list(refs)
+        given_refs = [refs.pop(0) for _ in given]
+        refs = refs[len(behind) :]
+        out, sems = refs[0], refs[-1]
+        row, column = (chunk * rows, 0) if axis == 0 else (0, chunk * wide)
+        copies = [
+            pltpu.make_async_copy(
+                w_hbm.at[pl.ds(row + i * step, step), pl.ds(column, wide)],
+                out.at[pl.ds(i * step, step)],
+                sems.at[i],
+            )
+            for i in range(blocks)
+        ]
+        for copy in copies:
+            copy.start()
+        for i, copy in enumerate(copies):
+            copy.wait()
+            if norms:
+                own = slice(i * step, (i + 1) * step)
+                part = jnp.zeros((step, 128), F32)
+                for c in range(0, wide, 128):
+                    x = out[own, c : c + 128].astype(F32)
+                    part = part + x * x
+                total = jnp.sum(part, axis=1, keepdims=True)
+                if given:
+                    total = total + given_refs[0][own, :]
+                refs[1][own, :] = jnp.sqrt(total + epsilon) if last else total
+
+    out_shape = [pltpu.VMEM(shape, weight.dtype)]
+    if norms:
+        out_shape.append(jax.ShapeDtypeStruct((rows, 1), F32))
+    return call(
+        body, out_shape, [pltpu.SemaphoreType.DMA((blocks,))], 6,
+        4096 * 2048 * 128, 2 * rows * wide,
+        [pltpu.with_memory_space_constraint(weight, pltpu.HBM)] + given + behind,
+        [pltpu.HBM] + [VMEM] * len(given) + [ANY] * len(behind),
+        [VMEM] * len(out_shape),
+    )
+
+
+def held(x):
+    return pltpu.with_memory_space_constraint(x, pltpu.VMEM)
+
+
+def encode(halves, weight, groups):
+    half, wide = halves[0].shape
+    rows = 2 * half
+    share = weight.shape[1] // groups
+
+    def body(a_ref, b_ref, w_ref, *refs):
+        x = refs[groups]
+        me = lax.axis_index("layer")
+        x[:half, :] = a_ref[...]
+        x[half:, :] = b_ref[...]
+        for k in list(range(1, groups)) + [0]:
+            at = pl.multiple_of((me ^ k) * share, share)
+            y = jnp.dot(x[...], w_ref[:, pl.ds(at, share)], preferred_element_type=F32)
+            refs[k][...] = y.astype(refs[k].dtype)
+
+    kinds = [BF16 if k else F32 for k in range(groups)]
+    args = [*halves, held(weight)]
+    return call(
+        body, [jax.ShapeDtypeStruct((rows, share), kind) for kind in kinds],
+        [pltpu.VMEM((rows, wide), BF16)], 8,
+        2 * rows * wide * share * groups, 2 * wide * share * groups,
+        args, [VMEM] * len(args), [VMEM] * groups,
+    )
+
+
+def rebuild(hiddens, weights):
+    groups = len(hiddens)
+    rows, share = hiddens[0].shape
+    half = rows // 2
+    wide = weights[0].shape[1]
+    total = wide * len(weights)
+    block = min(512, wide)
+
+    def body(*refs):
+        hidden_refs, w_refs = refs[:groups], refs[groups : groups + len(weights)]
+        keep, send, x = refs[groups + len(weights) :]
+        me = lax.axis_index("layer")
+        for k in range(groups):
+            at = pl.multiple_of((me ^ k) * share, share)
+            x[:, pl.ds(at, share)] = hidden_refs[k][...]
+        for c, w_ref in enumerate(w_refs):
+            for n in range(0, wide, block):
+                y = jnp.dot(x[...], w_ref[:, n : n + block], preferred_element_type=F32)
+                own = slice(c * wide + n, c * wide + n + block)
+                keep[:, own] = y[:half]
+                send[:, own] = y[half:].astype(BF16)
+
+    args = [*hiddens] + [held(weight) for weight in weights]
+    return call(
+        body,
+        [jax.ShapeDtypeStruct((half, total), F32), jax.ShapeDtypeStruct((half, total), BF16)],
+        [pltpu.VMEM((rows, share * groups), BF16)], 8,
+        2 * rows * total * share * groups, 2 * total * share * groups,
+        args, [VMEM] * len(args), [VMEM] * 2,
+    )
+
+
+def back_product(halves, weight, norm_column, groups, acc):
+    half, wide = halves[0].shape
+    rows = 2 * half
+    share = weight.shape[0] // groups
+    last = acc is not None
+
+    def body(a_ref, b_ref, w_ref, *refs):
+        others, outs, x = refs[: groups if last else 1], refs[-1 - groups : -1], refs[-1]
+        me = lax.axis_index("layer")
+        x[:, :half] = a_ref[...].T
+        x[:, half:] = b_ref[...].T
+        for k in list(range(1, groups)) + [0]:
+            at = pl.multiple_of((me ^ k) * share, share)
+            y = jnp.dot(w_ref[pl.ds(at, share), :], x[...], preferred_element_type=F32)
+            if last:
+                y = y + others[k][...]
+            else:
+                y = y + (LOSS_SCALE * SPARSITY) * others[0][pl.ds(at, share), :]
+            outs[k][...] = y.astype(outs[k].dtype)
+
+    kinds = [BF16 if k and last else F32 for k in range(groups)]
+    args = [*halves, held(weight)] + (acc if last else [norm_column])
+    return call(
+        body, [jax.ShapeDtypeStruct((share, rows), kind) for kind in kinds],
+        [pltpu.VMEM((wide, rows), BF16)], 8,
+        2 * rows * wide * share * groups, 2 * wide * share * groups,
+        args, [VMEM] * len(args), [VMEM] * groups,
+    )
+
+
+def prepare(hiddens, norm_column):
+    groups = len(hiddens)
+    rows, share = hiddens[0].shape
+
+    def body(*refs):
+        norm_ref, turned, scale = refs[groups:]
+        me = lax.axis_index("layer")
+        for k in range(groups):
+            h = refs[k][...].T
+            at = pl.multiple_of((me ^ k) * share, share)
+            own = slice(k * share, (k + 1) * share)
+            totals = jnp.sum(h.astype(F32), axis=1, keepdims=True)
+            turned[own, :] = h
+            scale[own, :] = LOSS_SCALE * SPARSITY * totals / norm_ref[pl.ds(at, share), :]
+
+    args = [*hiddens, norm_column]
+    return call(
+        body,
+        [
+            jax.ShapeDtypeStruct((groups * share, rows), BF16),
+            jax.ShapeDtypeStruct((groups * share, 1), F32),
+        ],
+        [], 6, 2 * 128 * 4096 * 512, 4 * groups * share * rows, args, [VMEM] * len(args), [VMEM] * 2,
+    )
+
+
+def decoder_gradient(turned, scale, halves, weight, chunk, chunks, groups, into):
+    latents, rows = turned.shape
+    half, wide = halves[0].shape
+    share = latents // groups
+    step = min(256, share)
+    per = share // step
+    slots = 6
+    block = min(1024, wide)
+
+    def body(turned_ref, scale_ref, a_ref, b_ref, w_ref, *refs):
+        out, errors, stage, sems = refs[-4:]
+        me = lax.axis_index("layer")
+        errors[:half, :] = a_ref[...]
+        errors[half:, :] = b_ref[...]
+
+        def place(i):
+            return pl.multiple_of((me ^ (i // per)) * share + lax.rem(i, per) * step, step)
+
+        def copy(i):
+            slot = lax.rem(i, slots)
+            return pltpu.make_async_copy(
+                stage.at[slot],
+                out.at[pl.ds(place(i), step), pl.ds(chunk * wide, wide)],
+                sems.at[slot],
+            )
+
+        def loop(i, carry):
+            own = pl.multiple_of(i * step, step)
+            slot = lax.rem(i, slots)
+
+            @pl.when(i >= slots)
+            def _():
+                copy(i - slots).wait()
+
+            for n in range(0, wide, block):
+                y = jnp.dot(
+                    turned_ref[pl.ds(own, step), :], errors[:, n : n + block],
+                    preferred_element_type=F32,
+                )
+                w = w_ref[pl.ds(place(i), step), n : n + block].astype(F32)
+                stage[slot, :, n : n + block] = (
+                    y + w * scale_ref[pl.ds(own, step), :]
+                ).astype(BF16)
+            copy(i).start()
+            return carry
+
+        trips = per * groups
+        lax.fori_loop(0, trips, loop, 0)
+        for i in range(max(0, trips - slots), trips):
+            copy(i).wait()
+
+    args = [turned, scale, *halves, held(weight)]
+    spaces = [VMEM] * len(args)
+    aliases = {}
+    if into is not None:
+        aliases = {len(args): 0}
+        args.append(into)
+        spaces.append(ANY)
+    return call(
+        body, [jax.ShapeDtypeStruct((latents, wide * chunks), BF16)],
+        [
+            pltpu.VMEM((rows, wide), BF16),
+            pltpu.VMEM((slots, step, wide), BF16),
+            pltpu.SemaphoreType.DMA((slots,)),
+        ], 16,
+        4 * rows * wide * latents, 2 * wide * latents,
+        args, spaces, [ANY], aliases,
+    )[0]
+
+
+def activate(own, arrived, bias):
+    rows, share = own.shape
+
+    def body(own_ref, *refs):
+        refs = list(refs)
+        hidden_ref, slopes_ref = refs[-2:]
+        preact = own_ref[...]
+        for ref in refs[:-3]:
+            preact = preact + ref[...].astype(F32)
+        at = pl.multiple_of(lax.axis_index("layer") * share, share)
+        preact = preact + refs[-3][:, pl.ds(at, share)]
+        hidden_ref[...] = (jax.nn.softplus(sharpness * preact) / sharpness).astype(BF16)
+        slopes_ref[...] = jax.nn.sigmoid(sharpness * preact).T
+
+    args = [own, *arrived, bias[None, :]]
+    return call(
+        body,
+        [jax.ShapeDtypeStruct((rows, share), BF16), jax.ShapeDtypeStruct((share, rows), F32)],
+        [], 4, 2 * 128 * 4096 * 256, 12 * rows * share, args, [VMEM] * len(args), [VMEM] * 2,
+    )
+
+
+def split_rows(keep, arrived, places):
+    half, wide = keep.shape
+    rows = half // places
+
+    def body(keep_ref, arrived_ref, *outs):
+        for k, out in enumerate(outs):
+            own = slice(k * rows, (k + 1) * rows)
+            y = keep_ref[own, :] + arrived_ref[own, :].astype(F32)
+            out[...] = y.astype(out.dtype)
+
+    kinds = [BF16 if k else F32 for k in range(places)]
+    return call(
+        body, [jax.ShapeDtypeStruct((rows, wide), kind) for kind in kinds],
+        [], 4, 2 * 128 * 4096 * 64, 8 * half * wide, [keep, arrived], [VMEM] * 2, [VMEM] * places,
+    )
+
+
+def error_value(own, arrived, bias, tokens, first):
+    rows, wide = own.shape
+
+    def body(own_ref, *refs):
+        bias_ref, tokens_ref, out = refs[-3:]
+        columns = slice(first, first + wide)
+        value = own_ref[...]
+        for ref in refs[:-3]:
+            value = value + ref[...].astype(F32)
+        value = value + bias_ref[:, columns] - tokens_ref[:, columns].astype(F32)
+        out[...] = (LOSS_SCALE * value).astype(BF16)
+
+    args = [own, *arrived, bias[None, :], tokens]
+    return call(
+        body, [jax.ShapeDtypeStruct((rows, wide), BF16)],
+        [], 4, 2 * 128 * 4096 * 64, 12 * rows * wide, args, [VMEM] * len(args), [VMEM],
+    )[0]
+
+
+def slope_product(own, arrived, slopes):
+    def body(own_ref, *refs):
+        summed = own_ref[...]
+        for ref in refs[:-2]:
+            summed = summed + ref[...].astype(F32)
+        refs[-1][...] = (summed * refs[-2][...]).astype(BF16)
+
+    args = [own, *arrived, slopes]
+    return call(
+        body, [jax.ShapeDtypeStruct(own.shape, BF16)],
+        [], 4, 2 * 128 * 4096 * 256, 12 * own.size, args, [VMEM] * len(args), [VMEM],
+    )[0]
+
+
+def turn_tokens(halves):
+    half, wide = halves[0].shape
+
+    def body(a_ref, b_ref, out):
+        out[:, :half] = a_ref[...].T
+        out[:, half:] = b_ref[...].T
+
+    return call(
+        body, [jax.ShapeDtypeStruct((wide, 2 * half), BF16)], [], 6,
+        2 * 128 * 4096 * 512, 4 * wide * half, [*halves], [VMEM] * 2, [VMEM],
+    )[0]
+
+
+def encoder_gradient(gradients, ks, turned, shape, into):
+    share, rows = gradients[0].shape
+    count = len(ks)
+    step = 1024
+    per = shape[0] // step
+    slots = min(8, per * count)
+
+    def body(*rest):
+        refs = list(rest)
+        grad_refs = [refs.pop(0) for _ in ks]
+        t_ref = refs.pop(0)
+        if into is not None:
+            refs.pop(0)
+        out, g, stage, sems = refs
+        me = lax.axis_index("layer")
+        copies = []
+        for i, k in enumerate(ks):
+            at = pl.multiple_of((me ^ k) * share, share)
+            g[...] = grad_refs[i][...].T
+            for r in range(per):
+                slot = len(copies) % slots
+                if len(copies) >= slots:
+                    copies[len(copies) - slots].wait()
+                y = jnp.dot(t_ref[r * step : (r + 1) * step, :], g[...], preferred_element_type=F32)
+                stage[slot] = y.astype(BF16)
+                copy = pltpu.make_async_copy(
+                    stage.at[slot],
+                    out.at[pl.ds(r * step, step), pl.ds(at, share)],
+                    sems.at[slot],
+                )
+                copy.start()
+                copies.append(copy)
+        for copy in copies[len(copies) - slots :]:
+            copy.wait()
+
+    args = [gradients[k] for k in ks] + [turned]
+    spaces = [VMEM] * len(args)
+    aliases = {}
+    if into is not None:
+        aliases = {len(args): 0}
+        args.append(into)
+        spaces.append(ANY)
+    return call(
+        body, [jax.ShapeDtypeStruct(shape, BF16)],
+        [
+            pltpu.VMEM((rows, share), BF16),
+            pltpu.VMEM((slots, step, share), BF16),
+            pltpu.SemaphoreType.DMA((slots,)),
+        ], 16,
+        4 * rows * shape[0] * share * count, 2 * shape[0] * share * count,
+        args, spaces, [ANY], aliases,
+    )[0]
+
+
+def shards(tokens, encoder_weight, encoder_bias, decoder_weight, decoder_bias):
+    _, width = tokens.shape
+    latents = encoder_weight.shape[1]
+    groups = lax.axis_size("layer")
+    places = lax.axis_size("latent") // 2
+    share = latents // groups
+    powers = groups & (groups - 1) == 0 and places & (places - 1) == 0
+    if width != D or share % 128 or width % (512 * CHUNKS) or not powers or places < 2:
+        return general(tokens, encoder_weight, encoder_bias, decoder_weight, decoder_bias)
+
+    def layer_move(x, k):
+        return lax.ppermute(x, "layer", [(i, i ^ k) for i in range(groups)])
+
+    def place_move(x, k):
+        pairs = [(2 * z + c, 2 * (z ^ k) + c) for z in range(places) for c in range(2)]
+        return lax.ppermute(x, "latent", pairs)
+
+    def core_move(x):
+        return lax.ppermute(x, "latent", [(i, i ^ 1) for i in range(2 * places)])
+
+    def spread(own):
+        moved = [place_move(own, k) for k in range(1, places)]
+        return jnp.concatenate([own] + moved, axis=0)
+
+    def exchange(xs):
+        return [layer_move(x, k) for k, x in enumerate(xs) if k]
+
+    encoder = hold(encoder_weight, 8, 0, 0, 1, [])[0]
+    mine = spread(tokens)
+    every = (mine, core_move(mine))
+    acc = encode(every, encoder, groups)
+
+    decoder, norm_column = [], "zero"
+    for c in range(CHUNKS):
+        held_c, norm_column = hold(
+            decoder_weight, 8, 1, c, CHUNKS, [acc[1]] if c == 0 else [], norm_column
+        )
+        decoder.append(held_c)
+    arrived = exchange(acc)
+    hidden, slopes = activate(acc[0], arrived, encoder_bias)
+    hiddens = [hidden] + exchange([hidden] * groups)
+    turned = turn_tokens(every)
+    hidden_turned, scale = prepare(hiddens, norm_column)
+    piece = width // CHUNKS
+    error_grads = []
+    for c in range(CHUNKS):
+        keep, send = rebuild(hiddens, [decoder[c]])
+        parts = split_rows(keep, core_move(send), places)
+        moved = [place_move(parts[k], k) for k in range(1, places)]
+        value = error_value(parts[0], moved, decoder_bias, tokens, c * piece)
+        mine = spread(value)
+        error_grads.append((mine, core_move(mine)))
+    back = None
+    for c in range(CHUNKS):
+        back = back_product(error_grads[c], decoder[c], norm_column, groups, back)
+    arrived = exchange(back)
+    grad = slope_product(back[0], arrived, slopes)
+    grads = [grad] + exchange([grad] * groups)
+    decoder_grad = None
+    for c in range(CHUNKS):
+        decoder_grad = decoder_gradient(
+            hidden_turned, scale, error_grads[c], decoder[c], c, CHUNKS, groups, decoder_grad
+        )
+    shape = encoder_weight.shape
+    encoder_grad = encoder_gradient(grads, [0], turned, shape, None)
+    encoder_grad = encoder_gradient(
+        grads, list(range(1, groups)), turned, shape, encoder_grad
+    )
+    return (encoder_grad, decoder_grad)
+
+
 def solution(mesh):
     placed = (
         P("latent", "layer"),
@@ -66,6 +538,7 @@
         P("latent", "layer"),
         P("layer"),
     )
+
     return jax.shard_map(
         shards,
         mesh=mesh,

time: 249 us -> 110 us (0.44)
  waiting for transfers between devices: 112 us -> 24.1 us
  matrix products: 51.3 us -> 0 us
  Pallas kernels: 0 us -> 43.1 us
  starting transfers between devices: 0.16 us -> 40.9 us
  blocking collectives: 35.3 us -> 0 us
  local copies, waits for them, and re-layouts: 23.2 us -> 1 us
  between operations: 13.9 us -> 1.11 us
  other arithmetic: 11.7 us -> 0.04 us
    dot_general x5 -> x0, matrix products: 51.3 us -> none  [the longest x1 12.4 us: shards(): lax.dot_general(error_grad, decoder_weight, (((1,), (1,)), ((), ())), pre...]
    pallas_call x0 -> x20, Pallas kernels: none -> 43.1 us  [call(): pl.pallas_call(body, in_specs=[pl.BlockSpec(memory_space=s) for s in spac...]
    psum x1 -> x0, waiting for transfers between devices: 42.5 us -> none  [shards(): lax.psum(jnp.dot(hidden, decoder_weight, preferred_element_type=jnp.float...]
    reduce_scatter x2 -> x0, waiting for transfers between devices: 42.4 us -> none  [the longest x1 26.9 us: shards(): lax.psum_scatter(partial_value, 'layer', scatter_dimension=1, tiled=True)]
    ppermute x0 -> x32, starting transfers between devices: none -> 40.9 us  [the longest x15 25.8 us: place_move(): return lax.ppermute(x, 'latent', pairs)]
    all_gather x1 -> x0, waiting for transfers between devices: 26.6 us -> none  [shards(): every_token = lax.all_gather(tokens, 'latent', axis=0, tiled=True)]
    ppermute x0 -> x32, waiting for transfers between devices: none -> 24.1 us  [the longest x15 15.8 us: place_move(): return lax.ppermute(x, 'latent', pairs)]
    unnamed x7 -> x9, local copies, waits for them, and re-layouts: 22.4 us -> 0.98 us
  transfers between devices with their start and end apart: 4 -> 32, of which waited for: 4 -> 10; matrix products, arithmetic and copies ran while one was open for 8% -> 1% of each run, Pallas kernels for 0% -> 28%
where the time goes in v1:
time: 110 us
  Pallas kernels  43.1 us (39%)
  starting transfers between devices  40.9 us (37%)
  waiting for transfers between devices  24.1 us (22%)
  between operations  1.11 us (1%)
    pallas_call x20, Pallas kernels, call(): pl.pallas_call(body, in_specs=[pl.BlockSpec(memory_space=s) for s in spac...  43.1 us
    ppermute x15, starting transfers between devices, place_move(): return lax.ppermute(x, 'latent', pairs)  25.8 us
    ppermute x15, waiting for transfers between devices, place_move(): return lax.ppermute(x, 'latent', pairs)  15.8 us
    ppermute x12, starting transfers between devices, layer_move(): return lax.ppermute(x, 'layer', [(i, i ^ k) for i in range(groups)])  14.2 us
    ppermute x12, waiting for transfers between devices, layer_move(): return lax.ppermute(x, 'layer', [(i, i ^ k) for i in range(groups)])  8.35 us
  transfers between devices with their start and end apart: 32, of which 10 were waited for; matrix products, arithmetic and copies ran while one was open for 1% of the time, Pallas kernels for 28%

profile of v1, /device:TPU:0, one launch (start us, length us, event | category | flops | bytes accessed | tf_op | source)
XLA Modules:
  0.0 110.3 jit_solution(3927709425919905255)
XLA Ops:
  0.6 5.1 %collective-permute-start.2 = (bf16[16,4096]{1,0:T(8,128)(2,1)}, bf16[16,4096]{1,0:T(8,128)(2,1)S(1)}, u32[]{:S(2)}, u32[]{:S(2)}) collective-permute-start(bf16[16,4096]{1,0:T(8,128)(2,1)} %refs_4_.3), channel_id=1, source_target_pairs={{0,6},{1,7},{2,4},{3,5},{4,2},{5,3},{6,0},{7,1},{8,14},{9,15},{10,... | collective-permute-start | bytes 393224 | tf_op jit(solution)/shard_map/ppermute | solution.py:477
  7.4 7.1 %collective-permute-done = bf16[16,4096]{1,0:T(8,128)(2,1)S(1)} collective-permute-done((bf16[16,4096]{1,0:T(8,128)(2,1)}, bf16[16,4096]{1,0:T(8,128)(2,1)S(1)}, u32[]{:S(2)}, u32[]{:S(2)}) %collective-permute-start) | collective-permute-done | bytes 131104 | tf_op jit(solution)/shard_map/ppermute | solution.py:477
  14.5 2.5 %collective-permute-done.1 = bf16[16,4096]{1,0:T(8,128)(2,1)S(1)} collective-permute-done((bf16[16,4096]{1,0:T(8,128)(2,1)}, bf16[16,4096]{1,0:T(8,128)(2,1)S(1)}, u32[]{:S(2)}, u32[]{:S(2)}) %collective-permute-start.1) | collective-permute-done | bytes 131104 | tf_op jit(solution)/shard_map/ppermute | solution.py:477
  17.2 5.9 %shard_map.68.w_ref = bf16[4096,2048]{1,0:T(8,128)(2,1)S(1)} custom-call(bf16[4096,2048]{1,0:T(8,128)(2,1)} %w_hbm.3), custom_call_target="tpu_custom_call" | custom-call | flops 1073741824 | bytes 16777216 | tf_op jit(solution)/shard_map/pallas_call | solution.py:71
  23.1 2.4 %shard_map.69 = (f32[128,512]{1,0:T(8,128)S(1)}, bf16[128,512]{1,0:T(8,128)(2,1)S(1)}, bf16[128,512]{1,0:T(8,128)(2,1)S(1)}, bf16[128,512]{1,0:T(8,128)(2,1)S(1)}) custom-call(bf16[64,4096]{1,0:T(8,128)(2,1)S(1)} %constant_dynamic-update-slice_fusion.a_ref, bf16[64,4096]{1,0:T(8,128)(2,1)S(1)} %collective-permute-done.3.b_ref, ...), custom_call_target="tpu_custom_call" | custom-call | flops 2147483648 | bytes 16777216 | tf_op jit(solution)/shard_map/pallas_call | solution.py:71
  25.6 1.6 %collective-permute-start.5 = (bf16[128,512]{1,0:T(8,128)(2,1)S(1)}, bf16[128,512]{1,0:T(8,128)(2,1)S(1)}, u32[]{:S(2)}, u32[]{:S(2)}) collective-permute-start(bf16[128,512]{1,0:T(8,128)(2,1)S(1)} %get-tuple-element.36), channel_id=1, source_target_pairs={{0,16},{8,24},{16,0},{24,8},{1,17},{9,25},{17,1},{25,9},{2,18},{10... | collective-permute-start | bytes 393224 | tf_op jit(solution)/shard_map/ppermute | solution.py:473
  29.1 5.1 %collective-permute-done.5.refs_1_ = bf16[128,512]{1,0:T(8,128)(2,1)S(1)} collective-permute-done((bf16[128,512]{1,0:T(8,128)(2,1)S(1)}, bf16[128,512]{1,0:T(8,128)(2,1)S(1)}, u32[]{:S(2)}, u32[]{:S(2)}) %collective-permute-start.5) | collective-permute-done | bytes 131104 | tf_op jit(solution)/shard_map/ppermute | solution.py:473
  35.9 2.5 %collective-permute-start.9 = (bf16[128,512]{1,0:T(8,128)(2,1)S(1)}, bf16[128,512]{1,0:T(8,128)(2,1)S(1)}, u32[]{:S(2)}, u32[]{:S(2)}) collective-permute-start(bf16[128,512]{1,0:T(8,128)(2,1)S(1)} %get-tuple-element.38.refs_0_), channel_id=1, source_target_pairs={{0,24},{8,16},{16,8},{24,0},{1,25},{9,17},{17,9},{25,1},{2,26},{10... | collective-permute-start | bytes 393224 | tf_op jit(solution)/shard_map/ppermute | solution.py:473
  39.4 3.8 %shard_map.71 = (bf16[2048,2048]{1,0:T(8,128)(2,1)S(1)}, f32[2048,1]{1,0:T(8,128)S(1)}) custom-call(bf16[2048,4096]{1,0:T(8,128)(2,1)} %w_hbm.5, bf16[128,512]{1,0:T(8,128)(2,1)S(1)} %get-tuple-element.35.refs_0_), custom_call_target="tpu_custom_call" | custom-call | flops 1073741824 | bytes 8388608 | tf_op jit(solution)/shard_map/pallas_call | solution.py:71
  43.2 3.8 %shard_map.72 = (bf16[2048,2048]{1,0:T(8,128)(2,1)S(1)}, f32[2048,1]{1,0:T(8,128)S(1)}) custom-call(bf16[2048,4096]{1,0:T(8,128)(2,1)} %w_hbm.5, f32[2048,1]{1,0:T(8,128)S(1)} %get-tuple-element.39.refs_0_), custom_call_target="tpu_custom_call" | custom-call | flops 1073741824 | bytes 8388608 | tf_op jit(solution)/shard_map/pallas_call | solution.py:71
  50.4 3.0 %collective-permute-start.20 = (bf16[16,2048]{1,0:T(8,128)(2,1)S(1)}, bf16[16,2048]{1,0:T(8,128)(2,1)S(1)}, u32[]{:S(2)}, u32[]{:S(2)}) collective-permute-start(bf16[16,2048]{1,0:T(8,128)(2,1)S(1)} %get-tuple-element.52), channel_id=1, source_target_pairs={{0,4},{1,5},{2,6},{3,7},{4,0},{5,1},{6,2},{7,3},{8,12},{9,13},{10,... | collective-permute-start | bytes 196616 | tf_op jit(solution)/shard_map/ppermute | solution.py:477
  54.9 3.0 %collective-permute-start.12 = (bf16[16,2048]{1,0:T(8,128)(2,1)S(1)}, bf16[16,2048]{1,0:T(8,128)(2,1)S(1)}, u32[]{:S(2)}, u32[]{:S(2)}) collective-permute-start(bf16[16,2048]{1,0:T(8,128)(2,1)S(1)} %get-tuple-element.45), channel_id=1, source_target_pairs={{0,4},{1,5},{2,6},{3,7},{4,0},{5,1},{6,2},{7,3},{8,12},{9,13},{10,... | collective-permute-start | bytes 196616 | tf_op jit(solution)/shard_map/ppermute | solution.py:477
  60.3 1.8 %collective-permute-start.24 = (bf16[16,2048]{1,0:T(8,128)(2,1)S(1)}, bf16[16,2048]{1,0:T(8,128)(2,1)S(1)}, u32[]{:S(2)}, u32[]{:S(2)}) collective-permute-start(bf16[16,2048]{1,0:T(8,128)(2,1)S(1)} %shard_map.78), channel_id=1, source_target_pairs={{0,6},{1,7},{2,4},{3,5},{4,2},{5,3},{6,0},{7,1},{8,14},{9,15},{10,... | collective-permute-start | bytes 196616 | tf_op jit(solution)/shard_map/ppermute | solution.py:477
  62.1 4.6 %collective-permute-start.23 = (bf16[16,2048]{1,0:T(8,128)(2,1)S(1)}, bf16[16,2048]{1,0:T(8,128)(2,1)S(1)}, u32[]{:S(2)}, u32[]{:S(2)}) collective-permute-start(bf16[16,2048]{1,0:T(8,128)(2,1)S(1)} %shard_map.78), channel_id=1, source_target_pairs={{0,4},{1,5},{2,6},{3,7},{4,0},{5,1},{6,2},{7,3},{8,12},{9,13},{10,... | collective-permute-start | bytes 196616 | tf_op jit(solution)/shard_map/ppermute | solution.py:477
  67.1 2.4 %collective-permute-start.16 = (bf16[16,2048]{1,0:T(8,128)(2,1)S(1)}, bf16[16,2048]{1,0:T(8,128)(2,1)S(1)}, u32[]{:S(2)}, u32[]{:S(2)}) collective-permute-start(bf16[16,2048]{1,0:T(8,128)(2,1)S(1)} %shard_map.75), channel_id=1, source_target_pairs={{0,6},{1,7},{2,4},{3,5},{4,2},{5,3},{6,0},{7,1},{8,14},{9,15},{10,... | collective-permute-start | bytes 196616 | tf_op jit(solution)/shard_map/ppermute | solution.py:477
  71.5 1.6 %collective-permute-done.23 = bf16[16,2048]{1,0:T(8,128)(2,1)S(1)} collective-permute-done((bf16[16,2048]{1,0:T(8,128)(2,1)S(1)}, bf16[16,2048]{1,0:T(8,128)(2,1)S(1)}, u32[]{:S(2)}, u32[]{:S(2)}) %collective-permute-start.23) | collective-permute-done | bytes 65568 | tf_op jit(solution)/shard_map/ppermute | solution.py:477
  74.6 2.1 %collective-permute-done.15 = bf16[16,2048]{1,0:T(8,128)(2,1)S(1)} collective-permute-done((bf16[16,2048]{1,0:T(8,128)(2,1)S(1)}, bf16[16,2048]{1,0:T(8,128)(2,1)S(1)}, u32[]{:S(2)}, u32[]{:S(2)}) %collective-permute-start.15) | collective-permute-done | bytes 65568 | tf_op jit(solution)/shard_map/ppermute | solution.py:477
  78.7 2.8 %shard_map.79 = (f32[512,128]{1,0:T(8,128)S(1)}, f32[512,128]{1,0:T(8,128)S(1)}, f32[512,128]{1,0:T(8,128)S(1)}, f32[512,128]{1,0:T(8,128)S(1)}) custom-call(bf16[64,2048]{1,0:T(8,128)(2,1)S(1)} %pad_maximum_fusion.1.a_ref, bf16[64,2048]{1,0:T(8,128)(2,1)S(1)} %collective-permute-done.25.b_ref, bf16[2048,2048]{1,0:T(8,128)(2,1)S(1)} %get-tuple-element.47.refs_4_.w_ref, ...), custom_call_target="tpu_custom_call" | custom-call | flops 1073741824 | bytes 8388608 | tf_op jit(solution)/shard_map/pallas_call | solution.py:71
  81.5 2.8 %shard_map.80 = (f32[512,128]{1,0:T(8,128)S(1)}, bf16[512,128]{1,0:T(8,128)(2,1)S(1)}, bf16[512,128]{1,0:T(8,128)(2,1)S(1)}, bf16[512,128]{1,0:T(8,128)(2,1)S(1)}) custom-call(bf16[64,2048]{1,0:T(8,128)(2,1)S(1)} %pad_maximum_fusion.a_ref, bf16[64,2048]{1,0:T(8,128)(2,1)S(1)} %collective-permute-done.17.b_ref, ...), custom_call_target="tpu_custom_call" | custom-call | flops 1073741824 | bytes 8388608 | tf_op jit(solution)/shard_map/pallas_call | solution.py:71
  87.8 4.5 %shard_map.86.refs_0_ = bf16[2048,4096]{1,0:T(8,128)(2,1)} custom-call(bf16[2048,128]{1,0:T(8,128)(2,1)S(1)} %get-tuple-element.64.turned_ref, f32[2048,1]{1,0:T(8,128)S(1)} %get-tuple-element.65.scale_ref, bf16[64,2048]{1,0:T(8,128)(2,1)S(1)} %pad_maximum_fusion.1.a_ref, bf16[64,2048]{1,0:T(8,128)(2,1)S(1)} %collective-permute-done.25.b_ref, ...), custom_call_target="tpu_custom_call" | custom-call | flops 2147483648 | bytes 8388608 | tf_op jit(solution)/shard_map/pallas_call | solution.py:71
  92.4 1.9 %collective-permute-done.27.refs_1_ = bf16[512,128]{1,0:T(8,128)(2,1)S(1)} collective-permute-done((bf16[512,128]{1,0:T(8,128)(2,1)S(1)}, bf16[512,128]{1,0:T(8,128)(2,1)S(1)}, u32[]{:S(2)}, u32[]{:S(2)}) %collective-permute-start.27) | collective-permute-done | bytes 131104 | tf_op jit(solution)/shard_map/ppermute | solution.py:473
  97.9 4.5 %shard_map.87 = bf16[2048,4096]{1,0:T(8,128)(2,1)} custom-call(bf16[2048,128]{1,0:T(8,128)(2,1)S(1)} %get-tuple-element.64.turned_ref, f32[2048,1]{1,0:T(8,128)S(1)} %get-tuple-element.65.scale_ref, bf16[64,2048]{1,0:T(8,128)(2,1)S(1)} %pad_maximum_fusion.a_ref, bf16[64,2048]{1,0:T(8,128)(2,1)S(1)} %collective-permute-done.17.b_ref, ...), custom_call_target="tpu_custom_call", output_to_operand_aliasing={{}: (5, {})} | custom-call | flops 2147483648 | bytes 8388608 | tf_op jit(solution)/shard_map/pallas_call | solution.py:71
  102.4 2.5 %shard_map.83.rest_4_ = bf16[4096,2048]{1,0:T(8,128)(2,1)} custom-call(bf16[512,128]{1,0:T(8,128)(2,1)S(1)} %shard_map.81.rest_0_, bf16[4096,128]{1,0:T(8,128)(2,1)S(1)} %shard_map.82.rest_1_.rest_3_), custom_call_target="tpu_custom_call" | custom-call | flops 1073741824 | bytes 4194304 | tf_op jit(solution)/shard_map/pallas_call | solution.py:71
  105.0 5.1 %shard_map.84 = bf16[4096,2048]{1,0:T(8,128)(2,1)} custom-call(bf16[512,128]{1,0:T(8,128)(2,1)S(1)} %collective-permute-done.29.rest_0_, bf16[512,128]{1,0:T(8,128)(2,1)S(1)} %collective-permute-done.30.rest_1_, bf16[512,128]{1,0:T(8,128)(2,1)S(1)} %collective-permute-done.31.rest_2_, ...), custom_call_target="tpu_custom_call", output_to_operand_aliasing={{}: (4, {})} | custom-call | flops 3221225472 | bytes 12582912 | tf_op jit(solution)/shard_map/pallas_call | solution.py:71
  (72 shorter events, 26.5 us)
Async XLA Ops:
  0.6 16.4 %collective-permute-start.2 = (bf16[16,4096]{1,0:T(8,128)(2,1)}, bf16[16,4096]{1,0:T(8,128)(2,1)S(1)}, u32[]{:S(2)}, u32[]{:S(2)}) collective-permute-start(bf16[16,4096]{1,0:T(8,128)(2,1)} %refs_4_.3), channel_id=1, source_target_pairs={{0,6},{1,7},{2,4},{3,5},{4,2},{5,3},{6,0},{7,1},{8,14},{9,15},{10,... | collective-permute-start | bytes 393224 | tf_op jit(solution)/shard_map/ppermute | solution.py:477
  5.8 11.3 %collective-permute-start.1 = (bf16[16,4096]{1,0:T(8,128)(2,1)}, bf16[16,4096]{1,0:T(8,128)(2,1)S(1)}, u32[]{:S(2)}, u32[]{:S(2)}) collective-permute-start(bf16[16,4096]{1,0:T(8,128)(2,1)} %refs_4_.3), channel_id=1, source_target_pairs={{0,4},{1,5},{2,6},{3,7},{4,0},{5,1},{6,2},{7,3},{8,12},{9,13},{10,... | collective-permute-start | bytes 393224 | tf_op jit(solution)/shard_map/ppermute | solution.py:477
  5.8 8.7 %collective-permute-start = (bf16[16,4096]{1,0:T(8,128)(2,1)}, bf16[16,4096]{1,0:T(8,128)(2,1)S(1)}, u32[]{:S(2)}, u32[]{:S(2)}) collective-permute-start(bf16[16,4096]{1,0:T(8,128)(2,1)} %refs_4_.3), channel_id=1, source_target_pairs={{0,2},{1,3},{2,0},{3,1},{4,6},{5,7},{6,4},{7,5},{8,10},{9,11},{10,... | collective-permute-start | bytes 393224 | tf_op jit(solution)/shard_map/ppermute | solution.py:477
  25.6 8.6 %collective-permute-start.5 = (bf16[128,512]{1,0:T(8,128)(2,1)S(1)}, bf16[128,512]{1,0:T(8,128)(2,1)S(1)}, u32[]{:S(2)}, u32[]{:S(2)}) collective-permute-start(bf16[128,512]{1,0:T(8,128)(2,1)S(1)} %get-tuple-element.36), channel_id=1, source_target_pairs={{0,16},{8,24},{16,0},{24,8},{1,17},{9,25},{17,1},{25,9},{2,18},{10... | collective-permute-start | bytes 393224 | tf_op jit(solution)/shard_map/ppermute | solution.py:473
  27.1 7.3 %collective-permute-start.6 = (bf16[128,512]{1,0:T(8,128)(2,1)S(1)}, bf16[128,512]{1,0:T(8,128)(2,1)S(1)}, u32[]{:S(2)}, u32[]{:S(2)}) collective-permute-start(bf16[128,512]{1,0:T(8,128)(2,1)S(1)} %get-tuple-element.37), channel_id=1, source_target_pairs={{0,24},{8,16},{16,8},{24,0},{1,25},{9,17},{17,9},{25,1},{2,26},{10... | collective-permute-start | bytes 393224 | tf_op jit(solution)/shard_map/ppermute | solution.py:473
  28.6 7.0 %collective-permute-start.4 = (bf16[128,512]{1,0:T(8,128)(2,1)S(1)}, bf16[128,512]{1,0:T(8,128)(2,1)S(1)}, u32[]{:S(2)}, u32[]{:S(2)}) collective-permute-start(bf16[128,512]{1,0:T(8,128)(2,1)S(1)} %get-tuple-element.35.refs_0_), channel_id=1, source_target_pairs={{0,8},{8,0},{16,24},{24,16},{1,9},{9,1},{17,25},{25,17},{2,10},{10... | collective-permute-start | bytes 393224 | tf_op jit(solution)/shard_map/ppermute | solution.py:473
  35.9 11.1 %collective-permute-start.9 = (bf16[128,512]{1,0:T(8,128)(2,1)S(1)}, bf16[128,512]{1,0:T(8,128)(2,1)S(1)}, u32[]{:S(2)}, u32[]{:S(2)}) collective-permute-start(bf16[128,512]{1,0:T(8,128)(2,1)S(1)} %get-tuple-element.38.refs_0_), channel_id=1, source_target_pairs={{0,24},{8,16},{16,8},{24,0},{1,25},{9,17},{17,9},{25,1},{2,26},{10... | collective-permute-start | bytes 393224 | tf_op jit(solution)/shard_map/ppermute | solution.py:473
  38.4 8.6 %collective-permute-start.8 = (bf16[128,512]{1,0:T(8,128)(2,1)S(1)}, bf16[128,512]{1,0:T(8,128)(2,1)S(1)}, u32[]{:S(2)}, u32[]{:S(2)}) collective-permute-start(bf16[128,512]{1,0:T(8,128)(2,1)S(1)} %get-tuple-element.38.refs_0_), channel_id=1, source_target_pairs={{0,16},{8,24},{16,0},{24,8},{1,17},{9,25},{17,1},{25,9},{2,18},{10... | collective-permute-start | bytes 393224 | tf_op jit(solution)/shard_map/ppermute | solution.py:473
  38.9 8.1 %collective-permute-start.7 = (bf16[128,512]{1,0:T(8,128)(2,1)S(1)}, bf16[128,512]{1,0:T(8,128)(2,1)S(1)}, u32[]{:S(2)}, u32[]{:S(2)}) collective-permute-start(bf16[128,512]{1,0:T(8,128)(2,1)S(1)} %get-tuple-element.38.refs_0_), channel_id=1, source_target_pairs={{0,8},{8,0},{16,24},{24,16},{1,9},{9,1},{17,25},{25,17},{2,10},{10... | collective-permute-start | bytes 393224 | tf_op jit(solution)/shard_map/ppermute | solution.py:473
  50.3 7.6 %collective-permute-start.19 = (bf16[16,2048]{1,0:T(8,128)(2,1)S(1)}, bf16[16,2048]{1,0:T(8,128)(2,1)S(1)}, u32[]{:S(2)}, u32[]{:S(2)}) collective-permute-start(bf16[16,2048]{1,0:T(8,128)(2,1)S(1)} %get-tuple-element.51), channel_id=1, source_target_pairs={{0,2},{1,3},{2,0},{3,1},{4,6},{5,7},{6,4},{7,5},{8,10},{9,11},{10,... | collective-permute-start | bytes 196616 | tf_op jit(solution)/shard_map/ppermute | solution.py:477
  50.4 8.9 %collective-permute-start.20 = (bf16[16,2048]{1,0:T(8,128)(2,1)S(1)}, bf16[16,2048]{1,0:T(8,128)(2,1)S(1)}, u32[]{:S(2)}, u32[]{:S(2)}) collective-permute-start(bf16[16,2048]{1,0:T(8,128)(2,1)S(1)} %get-tuple-element.52), channel_id=1, source_target_pairs={{0,4},{1,5},{2,6},{3,7},{4,0},{5,1},{6,2},{7,3},{8,12},{9,13},{10,... | collective-permute-start | bytes 196616 | tf_op jit(solution)/shard_map/ppermute | solution.py:477
  54.8 11.9 %collective-permute-start.11 = (bf16[16,2048]{1,0:T(8,128)(2,1)S(1)}, bf16[16,2048]{1,0:T(8,128)(2,1)S(1)}, u32[]{:S(2)}, u32[]{:S(2)}) collective-permute-start(bf16[16,2048]{1,0:T(8,128)(2,1)S(1)} %get-tuple-element.44), channel_id=1, source_target_pairs={{0,2},{1,3},{2,0},{3,1},{4,6},{5,7},{6,4},{7,5},{8,10},{9,11},{10,... | collective-permute-start | bytes 196616 | tf_op jit(solution)/shard_map/ppermute | solution.py:477
  54.9 12.1 %collective-permute-start.12 = (bf16[16,2048]{1,0:T(8,128)(2,1)S(1)}, bf16[16,2048]{1,0:T(8,128)(2,1)S(1)}, u32[]{:S(2)}, u32[]{:S(2)}) collective-permute-start(bf16[16,2048]{1,0:T(8,128)(2,1)S(1)} %get-tuple-element.45), channel_id=1, source_target_pairs={{0,4},{1,5},{2,6},{3,7},{4,0},{5,1},{6,2},{7,3},{8,12},{9,13},{10,... | collective-permute-start | bytes 196616 | tf_op jit(solution)/shard_map/ppermute | solution.py:477
  57.9 9.1 %collective-permute-start.13 = (bf16[16,2048]{1,0:T(8,128)(2,1)S(1)}, bf16[16,2048]{1,0:T(8,128)(2,1)S(1)}, u32[]{:S(2)}, u32[]{:S(2)}) collective-permute-start(bf16[16,2048]{1,0:T(8,128)(2,1)S(1)} %get-tuple-element.46), channel_id=1, source_target_pairs={{0,6},{1,7},{2,4},{3,5},{4,2},{5,3},{6,0},{7,1},{8,14},{9,15},{10,... | collective-permute-start | bytes 196616 | tf_op jit(solution)/shard_map/ppermute | solution.py:477
  60.3 10.4 %collective-permute-start.24 = (bf16[16,2048]{1,0:T(8,128)(2,1)S(1)}, bf16[16,2048]{1,0:T(8,128)(2,1)S(1)}, u32[]{:S(2)}, u32[]{:S(2)}) collective-permute-start(bf16[16,2048]{1,0:T(8,128)(2,1)S(1)} %shard_map.78), channel_id=1, source_target_pairs={{0,6},{1,7},{2,4},{3,5},{4,2},{5,3},{6,0},{7,1},{8,14},{9,15},{10,... | collective-permute-start | bytes 196616 | tf_op jit(solution)/shard_map/ppermute | solution.py:477
  62.1 11.1 %collective-permute-start.23 = (bf16[16,2048]{1,0:T(8,128)(2,1)S(1)}, bf16[16,2048]{1,0:T(8,128)(2,1)S(1)}, u32[]{:S(2)}, u32[]{:S(2)}) collective-permute-start(bf16[16,2048]{1,0:T(8,128)(2,1)S(1)} %shard_map.78), channel_id=1, source_target_pairs={{0,4},{1,5},{2,6},{3,7},{4,0},{5,1},{6,2},{7,3},{8,12},{9,13},{10,... | collective-permute-start | bytes 196616 | tf_op jit(solution)/shard_map/ppermute | solution.py:477
  67.1 7.5 %collective-permute-start.16 = (bf16[16,2048]{1,0:T(8,128)(2,1)S(1)}, bf16[16,2048]{1,0:T(8,128)(2,1)S(1)}, u32[]{:S(2)}, u32[]{:S(2)}) collective-permute-start(bf16[16,2048]{1,0:T(8,128)(2,1)S(1)} %shard_map.75), channel_id=1, source_target_pairs={{0,6},{1,7},{2,4},{3,5},{4,2},{5,3},{6,0},{7,1},{8,14},{9,15},{10,... | collective-permute-start | bytes 196616 | tf_op jit(solution)/shard_map/ppermute | solution.py:477
  69.5 7.2 %collective-permute-start.15 = (bf16[16,2048]{1,0:T(8,128)(2,1)S(1)}, bf16[16,2048]{1,0:T(8,128)(2,1)S(1)}, u32[]{:S(2)}, u32[]{:S(2)}) collective-permute-start(bf16[16,2048]{1,0:T(8,128)(2,1)S(1)} %shard_map.75), channel_id=1, source_target_pairs={{0,4},{1,5},{2,6},{3,7},{4,0},{5,1},{6,2},{7,3},{8,12},{9,13},{10,... | collective-permute-start | bytes 196616 | tf_op jit(solution)/shard_map/ppermute | solution.py:477
  84.3 8.1 %collective-permute-start.26 = (bf16[512,128]{1,0:T(8,128)(2,1)S(1)}, bf16[512,128]{1,0:T(8,128)(2,1)S(1)}, u32[]{:S(2)}, u32[]{:S(2)}) collective-permute-start(bf16[512,128]{1,0:T(8,128)(2,1)S(1)} %get-tuple-element.60), channel_id=1, source_target_pairs={{0,8},{8,0},{16,24},{24,16},{1,9},{9,1},{17,25},{25,17},{2,10},{10... | collective-permute-start | bytes 393224 | tf_op jit(solution)/shard_map/ppermute | solution.py:473
  85.8 8.4 %collective-permute-start.27 = (bf16[512,128]{1,0:T(8,128)(2,1)S(1)}, bf16[512,128]{1,0:T(8,128)(2,1)S(1)}, u32[]{:S(2)}, u32[]{:S(2)}) collective-permute-start(bf16[512,128]{1,0:T(8,128)(2,1)S(1)} %get-tuple-element.61), channel_id=1, source_target_pairs={{0,16},{8,24},{16,0},{24,8},{1,17},{9,25},{17,1},{25,9},{2,18},{10... | collective-permute-start | bytes 393224 | tf_op jit(solution)/shard_map/ppermute | solution.py:473
  87.4 6.9 %collective-permute-start.28 = (bf16[512,128]{1,0:T(8,128)(2,1)S(1)}, bf16[512,128]{1,0:T(8,128)(2,1)S(1)}, u32[]{:S(2)}, u32[]{:S(2)}) collective-permute-start(bf16[512,128]{1,0:T(8,128)(2,1)S(1)} %get-tuple-element.62), channel_id=1, source_target_pairs={{0,24},{8,16},{16,8},{24,0},{1,25},{9,17},{17,9},{25,1},{2,26},{10... | collective-permute-start | bytes 393224 | tf_op jit(solution)/shard_map/ppermute | solution.py:473
  94.3 10.6 %collective-permute-start.31 = (bf16[512,128]{1,0:T(8,128)(2,1)S(1)}, bf16[512,128]{1,0:T(8,128)(2,1)S(1)}, u32[]{:S(2)}, u32[]{:S(2)}) collective-permute-start(bf16[512,128]{1,0:T(8,128)(2,1)S(1)} %shard_map.81.rest_0_), channel_id=1, source_target_pairs={{0,24},{8,16},{16,8},{24,0},{1,25},{9,17},{17,9},{25,1},{2,26},{10... | collective-permute-start | bytes 393224 | tf_op jit(solution)/shard_map/ppermute | solution.py:473
  95.9 9.1 %collective-permute-start.30 = (bf16[512,128]{1,0:T(8,128)(2,1)S(1)}, bf16[512,128]{1,0:T(8,128)(2,1)S(1)}, u32[]{:S(2)}, u32[]{:S(2)}) collective-permute-start(bf16[512,128]{1,0:T(8,128)(2,1)S(1)} %shard_map.81.rest_0_), channel_id=1, source_target_pairs={{0,16},{8,24},{16,0},{24,8},{1,17},{9,25},{17,1},{25,9},{2,18},{10... | collective-permute-start | bytes 393224 | tf_op jit(solution)/shard_map/ppermute | solution.py:473
  97.1 7.9 %collective-permute-start.29 = (bf16[512,128]{1,0:T(8,128)(2,1)S(1)}, bf16[512,128]{1,0:T(8,128)(2,1)S(1)}, u32[]{:S(2)}, u32[]{:S(2)}) collective-permute-start(bf16[512,128]{1,0:T(8,128)(2,1)S(1)} %shard_map.81.rest_0_), channel_id=1, source_target_pairs={{0,8},{8,0},{16,24},{24,16},{1,9},{9,1},{17,25},{25,17},{2,10},{10... | collective-permute-start | bytes 393224 | tf_op jit(solution)/shard_map/ppermute | solution.py:473
  (11 other events, 89.1 us)

commit v2 on v1

--- a/solution.py
+++ b/solution.py
@@ -137,28 +137,28 @@
     return pltpu.with_memory_space_constraint(x, pltpu.VMEM)
 
 
-def encode(halves, weight, groups):
+def encode(halves, weight, groups, ks):
     half, wide = halves[0].shape
     rows = 2 * half
     share = weight.shape[1] // groups
 
     def body(a_ref, b_ref, w_ref, *refs):
-        x = refs[groups]
+        x = refs[-1]
         me = lax.axis_index("layer")
         x[:half, :] = a_ref[...]
         x[half:, :] = b_ref[...]
-        for k in list(range(1, groups)) + [0]:
+        for out, k in zip(refs, ks):
             at = pl.multiple_of((me ^ k) * share, share)
             y = jnp.dot(x[...], w_ref[:, pl.ds(at, share)], preferred_element_type=F32)
-            refs[k][...] = y.astype(refs[k].dtype)
-
-    kinds = [BF16 if k else F32 for k in range(groups)]
+            out[...] = y.astype(out.dtype)
+
+    kinds = [BF16 if k else F32 for k in ks]
     args = [*halves, held(weight)]
     return call(
         body, [jax.ShapeDtypeStruct((rows, share), kind) for kind in kinds],
         [pltpu.VMEM((rows, wide), BF16)], 8,
-        2 * rows * wide * share * groups, 2 * wide * share * groups,
-        args, [VMEM] * len(args), [VMEM] * groups,
+        2 * rows * wide * share * len(ks), 2 * wide * share * len(ks),
+        args, [VMEM] * len(args), [VMEM] * len(ks),
     )
 
 
@@ -250,13 +250,14 @@
     )
 
 
-def decoder_gradient(turned, scale, halves, weight, chunk, chunks, groups, into):
+def decoder_gradient(turned, scale, halves, weight, chunk, chunks, groups, ks, into):
     latents, rows = turned.shape
     half, wide = halves[0].shape
     share = latents // groups
     step = min(256, share)
     per = share // step
-    slots = 6
+    begin, end = per * ks[0], per * (ks[-1] + 1)
+    slots = min(6, end - begin)
     block = min(1024, wide)
 
     def body(turned_ref, scale_ref, a_ref, b_ref, w_ref, *refs):
@@ -280,7 +281,7 @@
             own = pl.multiple_of(i * step, step)
             slot = lax.rem(i, slots)
 
-            @pl.when(i >= slots)
+            @pl.when(i >= begin + slots)
             def _():
                 copy(i - slots).wait()
 
@@ -296,9 +297,8 @@
             copy(i).start()
             return carry
 
-        trips = per * groups
-        lax.fori_loop(0, trips, loop, 0)
-        for i in range(max(0, trips - slots), trips):
+        lax.fori_loop(begin, end, loop, 0, unroll=True)
+        for i in range(end - slots, end):
             copy(i).wait()
 
     args = [turned, scale, *halves, held(weight)]
@@ -315,7 +315,7 @@
             pltpu.VMEM((slots, step, wide), BF16),
             pltpu.SemaphoreType.DMA((slots,)),
         ], 16,
-        4 * rows * wide * latents, 2 * wide * latents,
+        4 * rows * wide * share * len(ks), 2 * wide * share * len(ks),
         args, spaces, [ANY], aliases,
     )[0]
 
@@ -483,13 +483,15 @@
         moved = [place_move(own, k) for k in range(1, places)]
         return jnp.concatenate([own] + moved, axis=0)
 
-    def exchange(xs):
-        return [layer_move(x, k) for k, x in enumerate(xs) if k]
+    def exchange(xs, first=0):
+        return [layer_move(x, k) for k, x in enumerate(xs, first) if k]
 
     encoder = hold(encoder_weight, 8, 0, 0, 1, [])[0]
     mine = spread(tokens)
     every = (mine, core_move(mine))
-    acc = encode(every, encoder, groups)
+    half = groups // 2
+    acc = encode(every, encoder, groups, list(range(half, groups)))
+    acc = encode(every, encoder, groups, list(range(half))) + acc
 
     decoder, norm_column = [], "zero"
     for c in range(CHUNKS):
@@ -497,7 +499,7 @@
             decoder_weight, 8, 1, c, CHUNKS, [acc[1]] if c == 0 else [], norm_column
         )
         decoder.append(held_c)
-    arrived = exchange(acc)
+    arrived = exchange(acc[:half]) + exchange(acc[half:], half)
     hidden, slopes = activate(acc[0], arrived, encoder_bias)
     hiddens = [hidden] + exchange([hidden] * groups)
     turned = turn_tokens(every)
@@ -518,9 +520,12 @@
     grad = slope_product(back[0], arrived, slopes)
     grads = [grad] + exchange([grad] * groups)
     decoder_grad = None
-    for c in range(CHUNKS):
+    pieces = [(c, range(groups)) for c in range(CHUNKS - 1)]
+    pieces += [(CHUNKS - 1, range(half)), (CHUNKS - 1, range(half, groups))]
+    for c, ks in pieces:
         decoder_grad = decoder_gradient(
-            hidden_turned, scale, error_grads[c], decoder[c], c, CHUNKS, groups, decoder_grad
+            hidden_turned, scale, error_grads[c], decoder[c], c, CHUNKS, groups, list(ks),
+            decoder_grad,
         )
     shape = encoder_weight.shape
     encoder_grad = encoder_gradient(grads, [0], turned, shape, None)

time: 110 us -> 108 us (0.982)
  waiting for transfers between devices: 24.1 us -> 21.2 us
    ppermute x12, waiting for transfers between devices: 8.35 us -> 5.45 us  [layer_move(): return lax.ppermute(x, 'layer', [(i, i ^ k) for i in range(groups)])]
    pallas_call x20 -> x22, Pallas kernels: 43.1 us -> 43.3 us  [call(): pl.pallas_call(body, in_specs=[pl.BlockSpec(memory_space=s) for s in spac...]
  transfers between devices with their start and end apart: 32 -> 32, of which waited for: 10 -> 11; matrix products, arithmetic and copies ran while one was open for 1% -> 1% of each run, Pallas kernels for 28% -> 30%
where the time goes in v2:
time: 108 us
  Pallas kernels  43.3 us (40%)
  starting transfers between devices  41 us (38%)
  waiting for transfers between devices  21.2 us (20%)
  between operations  1.14 us (1%)
    pallas_call x22, Pallas kernels, call(): pl.pallas_call(body, in_specs=[pl.BlockSpec(memory_space=s) for s in spac...  43.3 us
    ppermute x15, starting transfers between devices, place_move(): return lax.ppermute(x, 'latent', pairs)  25.8 us
    ppermute x15, waiting for transfers between devices, place_move(): return lax.ppermute(x, 'latent', pairs)  15.8 us
    ppermute x12, starting transfers between devices, layer_move(): return lax.ppermute(x, 'layer', [(i, i ^ k) for i in range(groups)])  14.3 us
    ppermute x12, waiting for transfers between devices, layer_move(): return lax.ppermute(x, 'layer', [(i, i ^ k) for i in range(groups)])  5.45 us
  transfers between devices with their start and end apart: 32, of which 11 were waited for; matrix products, arithmetic and copies ran while one was open for 1% of the time, Pallas kernels for 30%

profile of v2, /device:TPU:0, one launch (start us, length us, event | category | flops | bytes accessed | tf_op | source)
XLA Modules:
  0.0 107.6 jit_solution(16936988610484034805)
XLA Ops:
  0.6 5.1 %collective-permute-start.2 = (bf16[16,4096]{1,0:T(8,128)(2,1)}, bf16[16,4096]{1,0:T(8,128)(2,1)S(1)}, u32[]{:S(2)}, u32[]{:S(2)}) collective-permute-start(bf16[16,4096]{1,0:T(8,128)(2,1)} %refs_4_.3), channel_id=1, source_target_pairs={{0,6},{1,7},{2,4},{3,5},{4,2},{5,3},{6,0},{7,1},{8,14},{9,15},{10,... | collective-permute-start | bytes 393224 | tf_op jit(solution)/shard_map/ppermute | solution.py:477
  7.4 7.1 %collective-permute-done = bf16[16,4096]{1,0:T(8,128)(2,1)S(1)} collective-permute-done((bf16[16,4096]{1,0:T(8,128)(2,1)}, bf16[16,4096]{1,0:T(8,128)(2,1)S(1)}, u32[]{:S(2)}, u32[]{:S(2)}) %collective-permute-start) | collective-permute-done | bytes 131104 | tf_op jit(solution)/shard_map/ppermute | solution.py:477
  14.5 2.5 %collective-permute-done.1 = bf16[16,4096]{1,0:T(8,128)(2,1)S(1)} collective-permute-done((bf16[16,4096]{1,0:T(8,128)(2,1)}, bf16[16,4096]{1,0:T(8,128)(2,1)S(1)}, u32[]{:S(2)}, u32[]{:S(2)}) %collective-permute-start.1) | collective-permute-done | bytes 131104 | tf_op jit(solution)/shard_map/ppermute | solution.py:477
  17.2 5.9 %shard_map.68.w_ref = bf16[4096,2048]{1,0:T(8,128)(2,1)S(1)} custom-call(bf16[4096,2048]{1,0:T(8,128)(2,1)} %w_hbm.3), custom_call_target="tpu_custom_call" | custom-call | flops 1073741824 | bytes 16777216 | tf_op jit(solution)/shard_map/pallas_call | solution.py:71
  24.4 1.6 %collective-permute-start.5 = (bf16[128,512]{1,0:T(8,128)(2,1)S(1)}, bf16[128,512]{1,0:T(8,128)(2,1)S(1)}, u32[]{:S(2)}, u32[]{:S(2)}) collective-permute-start(bf16[128,512]{1,0:T(8,128)(2,1)S(1)} %get-tuple-element.36), channel_id=1, source_target_pairs={{0,16},{8,24},{16,0},{24,8},{1,17},{9,25},{17,1},{25,9},{2,18},{10... | collective-permute-start | bytes 393224 | tf_op jit(solution)/shard_map/ppermute | solution.py:473
  29.4 3.9 %collective-permute-done.5.refs_1_ = bf16[128,512]{1,0:T(8,128)(2,1)S(1)} collective-permute-done((bf16[128,512]{1,0:T(8,128)(2,1)S(1)}, bf16[128,512]{1,0:T(8,128)(2,1)S(1)}, u32[]{:S(2)}, u32[]{:S(2)}) %collective-permute-start.5) | collective-permute-done | bytes 131104 | tf_op jit(solution)/shard_map/ppermute | solution.py:473
  34.8 2.5 %collective-permute-start.9 = (bf16[128,512]{1,0:T(8,128)(2,1)S(1)}, bf16[128,512]{1,0:T(8,128)(2,1)S(1)}, u32[]{:S(2)}, u32[]{:S(2)}) collective-permute-start(bf16[128,512]{1,0:T(8,128)(2,1)S(1)} %get-tuple-element.38.refs_0_), channel_id=1, source_target_pairs={{0,24},{8,16},{16,8},{24,0},{1,25},{9,17},{17,9},{25,1},{2,26},{10... | collective-permute-start | bytes 393224 | tf_op jit(solution)/shard_map/ppermute | solution.py:473
  38.3 3.8 %shard_map.72 = (bf16[2048,2048]{1,0:T(8,128)(2,1)S(1)}, f32[2048,1]{1,0:T(8,128)S(1)}) custom-call(bf16[2048,4096]{1,0:T(8,128)(2,1)} %w_hbm.5, bf16[128,512]{1,0:T(8,128)(2,1)S(1)} %get-tuple-element.35.refs_0_), custom_call_target="tpu_custom_call" | custom-call | flops 1073741824 | bytes 8388608 | tf_op jit(solution)/shard_map/pallas_call | solution.py:71
  42.1 3.8 %shard_map.73 = (bf16[2048,2048]{1,0:T(8,128)(2,1)S(1)}, f32[2048,1]{1,0:T(8,128)S(1)}) custom-call(bf16[2048,4096]{1,0:T(8,128)(2,1)} %w_hbm.5, f32[2048,1]{1,0:T(8,128)S(1)} %get-tuple-element.39.refs_0_), custom_call_target="tpu_custom_call" | custom-call | flops 1073741824 | bytes 8388608 | tf_op jit(solution)/shard_map/pallas_call | solution.py:71
  49.3 3.0 %collective-permute-start.20 = (bf16[16,2048]{1,0:T(8,128)(2,1)S(1)}, bf16[16,2048]{1,0:T(8,128)(2,1)S(1)}, u32[]{:S(2)}, u32[]{:S(2)}) collective-permute-start(bf16[16,2048]{1,0:T(8,128)(2,1)S(1)} %get-tuple-element.52), channel_id=1, source_target_pairs={{0,4},{1,5},{2,6},{3,7},{4,0},{5,1},{6,2},{7,3},{8,12},{9,13},{10,... | collective-permute-start | bytes 196616 | tf_op jit(solution)/shard_map/ppermute | solution.py:477
  53.8 3.0 %collective-permute-start.12 = (bf16[16,2048]{1,0:T(8,128)(2,1)S(1)}, bf16[16,2048]{1,0:T(8,128)(2,1)S(1)}, u32[]{:S(2)}, u32[]{:S(2)}) collective-permute-start(bf16[16,2048]{1,0:T(8,128)(2,1)S(1)} %get-tuple-element.45), channel_id=1, source_target_pairs={{0,4},{1,5},{2,6},{3,7},{4,0},{5,1},{6,2},{7,3},{8,12},{9,13},{10,... | collective-permute-start | bytes 196616 | tf_op jit(solution)/shard_map/ppermute | solution.py:477
  59.2 1.8 %collective-permute-start.24 = (bf16[16,2048]{1,0:T(8,128)(2,1)S(1)}, bf16[16,2048]{1,0:T(8,128)(2,1)S(1)}, u32[]{:S(2)}, u32[]{:S(2)}) collective-permute-start(bf16[16,2048]{1,0:T(8,128)(2,1)S(1)} %shard_map.79), channel_id=1, source_target_pairs={{0,6},{1,7},{2,4},{3,5},{4,2},{5,3},{6,0},{7,1},{8,14},{9,15},{10,... | collective-permute-start | bytes 196616 | tf_op jit(solution)/shard_map/ppermute | solution.py:477
  61.0 4.6 %collective-permute-start.23 = (bf16[16,2048]{1,0:T(8,128)(2,1)S(1)}, bf16[16,2048]{1,0:T(8,128)(2,1)S(1)}, u32[]{:S(2)}, u32[]{:S(2)}) collective-permute-start(bf16[16,2048]{1,0:T(8,128)(2,1)S(1)} %shard_map.79), channel_id=1, source_target_pairs={{0,4},{1,5},{2,6},{3,7},{4,0},{5,1},{6,2},{7,3},{8,12},{9,13},{10,... | collective-permute-start | bytes 196616 | tf_op jit(solution)/shard_map/ppermute | solution.py:477
  66.0 2.4 %collective-permute-start.16 = (bf16[16,2048]{1,0:T(8,128)(2,1)S(1)}, bf16[16,2048]{1,0:T(8,128)(2,1)S(1)}, u32[]{:S(2)}, u32[]{:S(2)}) collective-permute-start(bf16[16,2048]{1,0:T(8,128)(2,1)S(1)} %shard_map.76), channel_id=1, source_target_pairs={{0,6},{1,7},{2,4},{3,5},{4,2},{5,3},{6,0},{7,1},{8,14},{9,15},{10,... | collective-permute-start | bytes 196616 | tf_op jit(solution)/shard_map/ppermute | solution.py:477
  70.4 1.6 %collective-permute-done.23 = bf16[16,2048]{1,0:T(8,128)(2,1)S(1)} collective-permute-done((bf16[16,2048]{1,0:T(8,128)(2,1)S(1)}, bf16[16,2048]{1,0:T(8,128)(2,1)S(1)}, u32[]{:S(2)}, u32[]{:S(2)}) %collective-permute-start.23) | collective-permute-done | bytes 65568 | tf_op jit(solution)/shard_map/ppermute | solution.py:477
  73.5 2.1 %collective-permute-done.15 = bf16[16,2048]{1,0:T(8,128)(2,1)S(1)} collective-permute-done((bf16[16,2048]{1,0:T(8,128)(2,1)S(1)}, bf16[16,2048]{1,0:T(8,128)(2,1)S(1)}, u32[]{:S(2)}, u32[]{:S(2)}) %collective-permute-start.15) | collective-permute-done | bytes 65568 | tf_op jit(solution)/shard_map/ppermute | solution.py:477
  77.6 2.8 %shard_map.80 = (f32[512,128]{1,0:T(8,128)S(1)}, f32[512,128]{1,0:T(8,128)S(1)}, f32[512,128]{1,0:T(8,128)S(1)}, f32[512,128]{1,0:T(8,128)S(1)}) custom-call(bf16[64,2048]{1,0:T(8,128)(2,1)S(1)} %pad_maximum_fusion.1.a_ref, bf16[64,2048]{1,0:T(8,128)(2,1)S(1)} %collective-permute-done.25.b_ref, bf16[2048,2048]{1,0:T(8,128)(2,1)S(1)} %get-tuple-element.47.refs_4_.w_ref, ...), custom_call_target="tpu_custom_call" | custom-call | flops 1073741824 | bytes 8388608 | tf_op jit(solution)/shard_map/pallas_call | solution.py:71
  80.4 2.8 %shard_map.81 = (f32[512,128]{1,0:T(8,128)S(1)}, bf16[512,128]{1,0:T(8,128)(2,1)S(1)}, bf16[512,128]{1,0:T(8,128)(2,1)S(1)}, bf16[512,128]{1,0:T(8,128)(2,1)S(1)}) custom-call(bf16[64,2048]{1,0:T(8,128)(2,1)S(1)} %pad_maximum_fusion.a_ref, bf16[64,2048]{1,0:T(8,128)(2,1)S(1)} %collective-permute-done.17.b_ref, ...), custom_call_target="tpu_custom_call" | custom-call | flops 1073741824 | bytes 8388608 | tf_op jit(solution)/shard_map/pallas_call | solution.py:71
  86.8 3.8 %shard_map.87.refs_0_ = bf16[2048,4096]{1,0:T(8,128)(2,1)} custom-call(bf16[2048,128]{1,0:T(8,128)(2,1)S(1)} %get-tuple-element.64.turned_ref, f32[2048,1]{1,0:T(8,128)S(1)} %get-tuple-element.65.scale_ref, bf16[64,2048]{1,0:T(8,128)(2,1)S(1)} %pad_maximum_fusion.1.a_ref, bf16[64,2048]{1,0:T(8,128)(2,1)S(1)} %collective-permute-done.25.b_ref, ...), custom_call_target="tpu_custom_call" | custom-call | flops 2147483648 | bytes 8388608 | tf_op jit(solution)/shard_map/pallas_call | solution.py:71
  90.6 2.5 %shard_map.88.refs_0_ = bf16[2048,4096]{1,0:T(8,128)(2,1)} custom-call(bf16[2048,128]{1,0:T(8,128)(2,1)S(1)} %get-tuple-element.64.turned_ref, f32[2048,1]{1,0:T(8,128)S(1)} %get-tuple-element.65.scale_ref, bf16[64,2048]{1,0:T(8,128)(2,1)S(1)} %pad_maximum_fusion.a_ref, ...), custom_call_target="tpu_custom_call", output_to_operand_aliasing={{}: (5, {})} | custom-call | flops 1073741824 | bytes 4194304 | tf_op jit(solution)/shard_map/pallas_call | solution.py:71
  93.3 2.4 %collective-permute-start.31 = (bf16[512,128]{1,0:T(8,128)(2,1)S(1)}, bf16[512,128]{1,0:T(8,128)(2,1)S(1)}, u32[]{:S(2)}, u32[]{:S(2)}) collective-permute-start(bf16[512,128]{1,0:T(8,128)(2,1)S(1)} %shard_map.82.rest_0_), channel_id=1, source_target_pairs={{0,24},{8,16},{16,8},{24,0},{1,25},{9,17},{17,9},{25,1},{2,26},{10... | collective-permute-start | bytes 393224 | tf_op jit(solution)/shard_map/ppermute | solution.py:473
  96.8 2.5 %shard_map.89 = bf16[2048,4096]{1,0:T(8,128)(2,1)} custom-call(bf16[2048,128]{1,0:T(8,128)(2,1)S(1)} %get-tuple-element.64.turned_ref, f32[2048,1]{1,0:T(8,128)S(1)} %get-tuple-element.65.scale_ref, bf16[64,2048]{1,0:T(8,128)(2,1)S(1)} %pad_maximum_fusion.a_ref, bf16[64,2048]{1,0:T(8,128)(2,1)S(1)} %collective-permute-done.17.b_ref, ...), custom_call_target="tpu_custom_call", output_to_operand_aliasing={{}: (5, {})} | custom-call | flops 1073741824 | bytes 4194304 | tf_op jit(solution)/shard_map/pallas_call | solution.py:71
  99.3 2.5 %shard_map.84.rest_4_ = bf16[4096,2048]{1,0:T(8,128)(2,1)} custom-call(bf16[512,128]{1,0:T(8,128)(2,1)S(1)} %shard_map.82.rest_0_, bf16[4096,128]{1,0:T(8,128)(2,1)S(1)} %shard_map.83.rest_1_.rest_3_), custom_call_target="tpu_custom_call" | custom-call | flops 1073741824 | bytes 4194304 | tf_op jit(solution)/shard_map/pallas_call | solution.py:71
  102.1 5.4 %shard_map.85 = bf16[4096,2048]{1,0:T(8,128)(2,1)} custom-call(bf16[512,128]{1,0:T(8,128)(2,1)S(1)} %collective-permute-done.29.rest_0_, bf16[512,128]{1,0:T(8,128)(2,1)S(1)} %collective-permute-done.30.rest_1_, bf16[512,128]{1,0:T(8,128)(2,1)S(1)} %collective-permute-done.31.rest_2_, ...), custom_call_target="tpu_custom_call", output_to_operand_aliasing={{}: (4, {})} | custom-call | flops 3221225472 | bytes 12582912 | tf_op jit(solution)/shard_map/pallas_call | solution.py:71
  (74 shorter events, 26.9 us)
Async XLA Ops:
  0.6 16.4 %collective-permute-start.2 = (bf16[16,4096]{1,0:T(8,128)(2,1)}, bf16[16,4096]{1,0:T(8,128)(2,1)S(1)}, u32[]{:S(2)}, u32[]{:S(2)}) collective-permute-start(bf16[16,4096]{1,0:T(8,128)(2,1)} %refs_4_.3), channel_id=1, source_target_pairs={{0,6},{1,7},{2,4},{3,5},{4,2},{5,3},{6,0},{7,1},{8,14},{9,15},{10,... | collective-permute-start | bytes 393224 | tf_op jit(solution)/shard_map/ppermute | solution.py:477
  5.8 11.3 %collective-permute-start.1 = (bf16[16,4096]{1,0:T(8,128)(2,1)}, bf16[16,4096]{1,0:T(8,128)(2,1)S(1)}, u32[]{:S(2)}, u32[]{:S(2)}) collective-permute-start(bf16[16,4096]{1,0:T(8,128)(2,1)} %refs_4_.3), channel_id=1, source_target_pairs={{0,4},{1,5},{2,6},{3,7},{4,0},{5,1},{6,2},{7,3},{8,12},{9,13},{10,... | collective-permute-start | bytes 393224 | tf_op jit(solution)/shard_map/ppermute | solution.py:477
  5.8 8.7 %collective-permute-start = (bf16[16,4096]{1,0:T(8,128)(2,1)}, bf16[16,4096]{1,0:T(8,128)(2,1)S(1)}, u32[]{:S(2)}, u32[]{:S(2)}) collective-permute-start(bf16[16,4096]{1,0:T(8,128)(2,1)} %refs_4_.3), channel_id=1, source_target_pairs={{0,2},{1,3},{2,0},{3,1},{4,6},{5,7},{6,4},{7,5},{8,10},{9,11},{10,... | collective-permute-start | bytes 393224 | tf_op jit(solution)/shard_map/ppermute | solution.py:477
  24.4 8.8 %collective-permute-start.5 = (bf16[128,512]{1,0:T(8,128)(2,1)S(1)}, bf16[128,512]{1,0:T(8,128)(2,1)S(1)}, u32[]{:S(2)}, u32[]{:S(2)}) collective-permute-start(bf16[128,512]{1,0:T(8,128)(2,1)S(1)} %get-tuple-element.36), channel_id=1, source_target_pairs={{0,16},{8,24},{16,0},{24,8},{1,17},{9,25},{17,1},{25,9},{2,18},{10... | collective-permute-start | bytes 393224 | tf_op jit(solution)/shard_map/ppermute | solution.py:473
  26.0 7.2 %collective-permute-start.6 = (bf16[128,512]{1,0:T(8,128)(2,1)S(1)}, bf16[128,512]{1,0:T(8,128)(2,1)S(1)}, u32[]{:S(2)}, u32[]{:S(2)}) collective-permute-start(bf16[128,512]{1,0:T(8,128)(2,1)S(1)} %get-tuple-element.37), channel_id=1, source_target_pairs={{0,24},{8,16},{16,8},{24,0},{1,25},{9,17},{17,9},{25,1},{2,26},{10... | collective-permute-start | bytes 393224 | tf_op jit(solution)/shard_map/ppermute | solution.py:473
  34.8 11.1 %collective-permute-start.9 = (bf16[128,512]{1,0:T(8,128)(2,1)S(1)}, bf16[128,512]{1,0:T(8,128)(2,1)S(1)}, u32[]{:S(2)}, u32[]{:S(2)}) collective-permute-start(bf16[128,512]{1,0:T(8,128)(2,1)S(1)} %get-tuple-element.38.refs_0_), channel_id=1, source_target_pairs={{0,24},{8,16},{16,8},{24,0},{1,25},{9,17},{17,9},{25,1},{2,26},{10... | collective-permute-start | bytes 393224 | tf_op jit(solution)/shard_map/ppermute | solution.py:473
  37.3 8.6 %collective-permute-start.8 = (bf16[128,512]{1,0:T(8,128)(2,1)S(1)}, bf16[128,512]{1,0:T(8,128)(2,1)S(1)}, u32[]{:S(2)}, u32[]{:S(2)}) collective-permute-start(bf16[128,512]{1,0:T(8,128)(2,1)S(1)} %get-tuple-element.38.refs_0_), channel_id=1, source_target_pairs={{0,16},{8,24},{16,0},{24,8},{1,17},{9,25},{17,1},{25,9},{2,18},{10... | collective-permute-start | bytes 393224 | tf_op jit(solution)/shard_map/ppermute | solution.py:473
  37.8 8.1 %collective-permute-start.7 = (bf16[128,512]{1,0:T(8,128)(2,1)S(1)}, bf16[128,512]{1,0:T(8,128)(2,1)S(1)}, u32[]{:S(2)}, u32[]{:S(2)}) collective-permute-start(bf16[128,512]{1,0:T(8,128)(2,1)S(1)} %get-tuple-element.38.refs_0_), channel_id=1, source_target_pairs={{0,8},{8,0},{16,24},{24,16},{1,9},{9,1},{17,25},{25,17},{2,10},{10... | collective-permute-start | bytes 393224 | tf_op jit(solution)/shard_map/ppermute | solution.py:473
  49.2 7.6 %collective-permute-start.19 = (bf16[16,2048]{1,0:T(8,128)(2,1)S(1)}, bf16[16,2048]{1,0:T(8,128)(2,1)S(1)}, u32[]{:S(2)}, u32[]{:S(2)}) collective-permute-start(bf16[16,2048]{1,0:T(8,128)(2,1)S(1)} %get-tuple-element.51), channel_id=1, source_target_pairs={{0,2},{1,3},{2,0},{3,1},{4,6},{5,7},{6,4},{7,5},{8,10},{9,11},{10,... | collective-permute-start | bytes 196616 | tf_op jit(solution)/shard_map/ppermute | solution.py:477
  49.3 8.9 %collective-permute-start.20 = (bf16[16,2048]{1,0:T(8,128)(2,1)S(1)}, bf16[16,2048]{1,0:T(8,128)(2,1)S(1)}, u32[]{:S(2)}, u32[]{:S(2)}) collective-permute-start(bf16[16,2048]{1,0:T(8,128)(2,1)S(1)} %get-tuple-element.52), channel_id=1, source_target_pairs={{0,4},{1,5},{2,6},{3,7},{4,0},{5,1},{6,2},{7,3},{8,12},{9,13},{10,... | collective-permute-start | bytes 196616 | tf_op jit(solution)/shard_map/ppermute | solution.py:477
  52.3 6.8 %collective-permute-start.21 = (bf16[16,2048]{1,0:T(8,128)(2,1)S(1)}, bf16[16,2048]{1,0:T(8,128)(2,1)S(1)}, u32[]{:S(2)}, u32[]{:S(2)}) collective-permute-start(bf16[16,2048]{1,0:T(8,128)(2,1)S(1)} %get-tuple-element.53), channel_id=1, source_target_pairs={{0,6},{1,7},{2,4},{3,5},{4,2},{5,3},{6,0},{7,1},{8,14},{9,15},{10,... | collective-permute-start | bytes 196616 | tf_op jit(solution)/shard_map/ppermute | solution.py:477
  53.7 11.9 %collective-permute-start.11 = (bf16[16,2048]{1,0:T(8,128)(2,1)S(1)}, bf16[16,2048]{1,0:T(8,128)(2,1)S(1)}, u32[]{:S(2)}, u32[]{:S(2)}) collective-permute-start(bf16[16,2048]{1,0:T(8,128)(2,1)S(1)} %get-tuple-element.44), channel_id=1, source_target_pairs={{0,2},{1,3},{2,0},{3,1},{4,6},{5,7},{6,4},{7,5},{8,10},{9,11},{10,... | collective-permute-start | bytes 196616 | tf_op jit(solution)/shard_map/ppermute | solution.py:477
  53.8 12.1 %collective-permute-start.12 = (bf16[16,2048]{1,0:T(8,128)(2,1)S(1)}, bf16[16,2048]{1,0:T(8,128)(2,1)S(1)}, u32[]{:S(2)}, u32[]{:S(2)}) collective-permute-start(bf16[16,2048]{1,0:T(8,128)(2,1)S(1)} %get-tuple-element.45), channel_id=1, source_target_pairs={{0,4},{1,5},{2,6},{3,7},{4,0},{5,1},{6,2},{7,3},{8,12},{9,13},{10,... | collective-permute-start | bytes 196616 | tf_op jit(solution)/shard_map/ppermute | solution.py:477
  56.8 9.1 %collective-permute-start.13 = (bf16[16,2048]{1,0:T(8,128)(2,1)S(1)}, bf16[16,2048]{1,0:T(8,128)(2,1)S(1)}, u32[]{:S(2)}, u32[]{:S(2)}) collective-permute-start(bf16[16,2048]{1,0:T(8,128)(2,1)S(1)} %get-tuple-element.46), channel_id=1, source_target_pairs={{0,6},{1,7},{2,4},{3,5},{4,2},{5,3},{6,0},{7,1},{8,14},{9,15},{10,... | collective-permute-start | bytes 196616 | tf_op jit(solution)/shard_map/ppermute | solution.py:477
  59.2 10.4 %collective-permute-start.24 = (bf16[16,2048]{1,0:T(8,128)(2,1)S(1)}, bf16[16,2048]{1,0:T(8,128)(2,1)S(1)}, u32[]{:S(2)}, u32[]{:S(2)}) collective-permute-start(bf16[16,2048]{1,0:T(8,128)(2,1)S(1)} %shard_map.79), channel_id=1, source_target_pairs={{0,6},{1,7},{2,4},{3,5},{4,2},{5,3},{6,0},{7,1},{8,14},{9,15},{10,... | collective-permute-start | bytes 196616 | tf_op jit(solution)/shard_map/ppermute | solution.py:477
  61.0 11.1 %collective-permute-start.23 = (bf16[16,2048]{1,0:T(8,128)(2,1)S(1)}, bf16[16,2048]{1,0:T(8,128)(2,1)S(1)}, u32[]{:S(2)}, u32[]{:S(2)}) collective-permute-start(bf16[16,2048]{1,0:T(8,128)(2,1)S(1)} %shard_map.79), channel_id=1, source_target_pairs={{0,4},{1,5},{2,6},{3,7},{4,0},{5,1},{6,2},{7,3},{8,12},{9,13},{10,... | collective-permute-start | bytes 196616 | tf_op jit(solution)/shard_map/ppermute | solution.py:477
  65.6 6.5 %collective-permute-start.22 = (bf16[16,2048]{1,0:T(8,128)(2,1)S(1)}, bf16[16,2048]{1,0:T(8,128)(2,1)S(1)}, u32[]{:S(2)}, u32[]{:S(2)}) collective-permute-start(bf16[16,2048]{1,0:T(8,128)(2,1)S(1)} %shard_map.79), channel_id=1, source_target_pairs={{0,2},{1,3},{2,0},{3,1},{4,6},{5,7},{6,4},{7,5},{8,10},{9,11},{10,... | collective-permute-start | bytes 196616 | tf_op jit(solution)/shard_map/ppermute | solution.py:477
  66.0 7.5 %collective-permute-start.16 = (bf16[16,2048]{1,0:T(8,128)(2,1)S(1)}, bf16[16,2048]{1,0:T(8,128)(2,1)S(1)}, u32[]{:S(2)}, u32[]{:S(2)}) collective-permute-start(bf16[16,2048]{1,0:T(8,128)(2,1)S(1)} %shard_map.76), channel_id=1, source_target_pairs={{0,6},{1,7},{2,4},{3,5},{4,2},{5,3},{6,0},{7,1},{8,14},{9,15},{10,... | collective-permute-start | bytes 196616 | tf_op jit(solution)/shard_map/ppermute | solution.py:477
  68.4 7.2 %collective-permute-start.15 = (bf16[16,2048]{1,0:T(8,128)(2,1)S(1)}, bf16[16,2048]{1,0:T(8,128)(2,1)S(1)}, u32[]{:S(2)}, u32[]{:S(2)}) collective-permute-start(bf16[16,2048]{1,0:T(8,128)(2,1)S(1)} %shard_map.76), channel_id=1, source_target_pairs={{0,4},{1,5},{2,6},{3,7},{4,0},{5,1},{6,2},{7,3},{8,12},{9,13},{10,... | collective-permute-start | bytes 196616 | tf_op jit(solution)/shard_map/ppermute | solution.py:477
  83.2 9.8 %collective-permute-start.26 = (bf16[512,128]{1,0:T(8,128)(2,1)S(1)}, bf16[512,128]{1,0:T(8,128)(2,1)S(1)}, u32[]{:S(2)}, u32[]{:S(2)}) collective-permute-start(bf16[512,128]{1,0:T(8,128)(2,1)S(1)} %get-tuple-element.60), channel_id=1, source_target_pairs={{0,8},{8,0},{16,24},{24,16},{1,9},{9,1},{17,25},{25,17},{2,10},{10... | collective-permute-start | bytes 393224 | tf_op jit(solution)/shard_map/ppermute | solution.py:473
  84.8 8.4 %collective-permute-start.27 = (bf16[512,128]{1,0:T(8,128)(2,1)S(1)}, bf16[512,128]{1,0:T(8,128)(2,1)S(1)}, u32[]{:S(2)}, u32[]{:S(2)}) collective-permute-start(bf16[512,128]{1,0:T(8,128)(2,1)S(1)} %get-tuple-element.61), channel_id=1, source_target_pairs={{0,16},{8,24},{16,0},{24,8},{1,17},{9,25},{17,1},{25,9},{2,18},{10... | collective-permute-start | bytes 393224 | tf_op jit(solution)/shard_map/ppermute | solution.py:473
  86.3 6.9 %collective-permute-start.28 = (bf16[512,128]{1,0:T(8,128)(2,1)S(1)}, bf16[512,128]{1,0:T(8,128)(2,1)S(1)}, u32[]{:S(2)}, u32[]{:S(2)}) collective-permute-start(bf16[512,128]{1,0:T(8,128)(2,1)S(1)} %get-tuple-element.62), channel_id=1, source_target_pairs={{0,24},{8,16},{16,8},{24,0},{1,25},{9,17},{17,9},{25,1},{2,26},{10... | collective-permute-start | bytes 393224 | tf_op jit(solution)/shard_map/ppermute | solution.py:473
  93.3 8.6 %collective-permute-start.31 = (bf16[512,128]{1,0:T(8,128)(2,1)S(1)}, bf16[512,128]{1,0:T(8,128)(2,1)S(1)}, u32[]{:S(2)}, u32[]{:S(2)}) collective-permute-start(bf16[512,128]{1,0:T(8,128)(2,1)S(1)} %shard_map.82.rest_0_), channel_id=1, source_target_pairs={{0,24},{8,16},{16,8},{24,0},{1,25},{9,17},{17,9},{25,1},{2,26},{10... | collective-permute-start | bytes 393224 | tf_op jit(solution)/shard_map/ppermute | solution.py:473
  95.7 6.3 %collective-permute-start.30 = (bf16[512,128]{1,0:T(8,128)(2,1)S(1)}, bf16[512,128]{1,0:T(8,128)(2,1)S(1)}, u32[]{:S(2)}, u32[]{:S(2)}) collective-permute-start(bf16[512,128]{1,0:T(8,128)(2,1)S(1)} %shard_map.82.rest_0_), channel_id=1, source_target_pairs={{0,16},{8,24},{16,0},{24,8},{1,17},{9,25},{17,1},{25,9},{2,18},{10... | collective-permute-start | bytes 393224 | tf_op jit(solution)/shard_map/ppermute | solution.py:473
  (11 other events, 86.3 us)
